TPU v7x, 256 devices: a whole 4x4x8 slice. The times are simulated.
256 devices in a mesh: dp: 64 (over z, y, core), pp: 4 (over x).
Axes of the slice: x: 4, y: 4, z: 8, core: 2. Of those that a mesh axis runs over, the one named last changes fastest.
Arguments:
- x_in: bfloat16 [2, 64, 197, 768], P(None, 'dp')
- grad_out: bfloat16 [2, 64, 197, 768], P(None, 'dp')
- vectors: bfloat16 [4, 9, 768], P('pp')
- w_qkv: bfloat16 [4, 768, 2304], P('pp')
- w_proj: bfloat16 [4, 12, 64, 768], P('pp')
- w_fc1: bfloat16 [4, 768, 3072], P('pp')
- b_fc1: bfloat16 [4, 3072], P('pp')
- w_fc2: bfloat16 [4, 3072, 768], P('pp')
Outputs:
- output 1: bfloat16 [4, 2, 64, 197, 768], P('pp', None, 'dp')
- output 2: bfloat16 [4, 2, 64, 197, 768], P('pp', None, 'dp')
- output 3: float32 [4, 9, 768], P('pp')
- output 4: float32 [4, 768, 2304], P('pp')
- output 5: float32 [4, 12, 64, 768], P('pp')
- output 6: float32 [4, 768, 3072], P('pp')
- output 7: float32 [4, 3072], P('pp')
- output 8: float32 [4, 3072, 768], P('pp')
All inputs are finite; a program needn't handle non-finite values.
Results may differ from a plain program's by a relative error of at most 0.02.
Values are sent between devices in bfloat16 or wider.
A program may use at most 768 MiB of HBM per device.

v0:
```python
import functools
import heapq
import math
import jax
import jax.numpy as jnp
from jax import lax
from jax.experimental import pallas as pl
from jax.experimental.pallas import tpu as pltpu
from jax.sharding import PartitionSpec as P

MESH = pl.DeviceIdType.MESH
F32 = jnp.float32
BF16 = jnp.bfloat16
TOK = 208
KEYS = 256
LANES = 128
SHIFT = 6200
PAIRS = 3


def dot_nn(a, b):
    return lax.dot_general(a, b, (((1,), (0,)), ((), ())), preferred_element_type=F32)


def dot_nt(a, b):
    return lax.dot_general(a, b, (((1,), (1,)), ((), ())), preferred_element_type=F32)


def dot_tn(a, b):
    return lax.dot_general(a, b, (((0,), (0,)), ((), ())), preferred_element_type=F32)


def rounded(x):
    return x.astype(BF16).astype(F32)


def aligned(start, size):
    return pl.ds(pl.multiple_of(start, LANES), size)


def pipeline_kernel(cfg, x_in, go_in, vec_ref, bf1_ref, wqkv_in, wproj_in, w1_in, w2_in,
                    so_out, sg_out, xa1, xa2, xo, xf, dqkv_out, dz_out, dr_out, gy_out, vec_out,
                    wqkv, wproj, w1, w2, wqkv_t, wproj_t, w1_t, w2_t, xt, hbuf, gbuf, obuf, gibuf, a1, qkv, att, res, a2, zact, fact, prob, stats,
                    dz, dres, datt, dqkv, vsum,
                    w_sem, in_sem, send_sem, recv_sem, loc_sem, psend_sem, precv_sem, vec_sem):
    seq, stages, n_micro = cfg
    width = wproj.shape[0]
    mlp = w1.shape[1]
    heads = width // 64
    half_qkv, half_mlp, half_w = 3 * width // 2, mlp // 2, width // 2
    dp = lax.axis_index('dp')
    stage = lax.axis_index('pp')
    core = lax.rem(dp, 2)
    mate = dp + 1 - 2 * core
    other = 1 - core
    last = stages - 1
    nxt = lax.rem(stage + 1, stages)
    prv = lax.rem(stage + stages - 1, stages)

    loads = [pltpu.make_async_copy(src, dst, w_sem.at[i])
             for i, (src, dst) in enumerate(((wqkv_in, wqkv), (wproj_in, wproj), (w1_in, w1), (w2_in, w2)))]

    def x_load(m):
        return pltpu.make_async_copy(x_in.at[m], hbuf.at[m], in_sem.at[m])

    def g_load(m):
        return pltpu.make_async_copy(go_in.at[m], gbuf.at[m], in_sem.at[n_micro + m])

    @pl.when(stage == 0)
    def _():
        for m in range(n_micro):
            x_load(m).start()
    for ld in loads:
        ld.start()

    @pl.when(stage == last)
    def _():
        for m in range(n_micro):
            g_load(m).start()

    @pl.when((stage == 0) & (core == 1))
    def _():
        pl.delay(SHIFT)

    barrier = pltpu.get_barrier_semaphore()
    pl.semaphore_signal(barrier, inc=1, device_id={'pp': nxt}, device_id_type=MESH)
    pl.semaphore_signal(barrier, inc=1, device_id={'pp': prv}, device_id_type=MESH)
    pl.semaphore_signal(barrier, inc=1, device_id={'dp': mate}, device_id_type=MESH)

    qkv[:, TOK:, :] = jnp.zeros((n_micro, KEYS - TOK, 3 * width), BF16)
    vsum[...] = jnp.zeros(vsum.shape, F32)
    pl.semaphore_wait(barrier, 3)

    def fwd_copy(m):
        return pltpu.make_async_remote_copy(obuf.at[m], hbuf.at[m], send_sem.at[m], recv_sem.at[m],
                                            device_id={'pp': nxt}, device_id_type=MESH)

    def bwd_copy(m):
        return pltpu.make_async_remote_copy(gibuf.at[m], gbuf.at[m], send_sem.at[n_micro + m], recv_sem.at[n_micro + m],
                                            device_id={'pp': prv}, device_id_type=MESH)

    def local(src, dst, m, i):
        return pltpu.make_async_copy(src, dst, loc_sem.at[m, i])

    def to_mate(src, dst, m, i):
        return pltpu.make_async_remote_copy(src, dst, psend_sem.at[m, i], precv_sem.at[m, i],
                                            device_id={'dp': mate}, device_id_type=MESH)

    def fwd_exports(m):
        own, fore = [pl.ds(pl.multiple_of(3 * width + c * half_mlp, LANES), half_mlp) for c in (core, other)]
        first, second, third = [slice(i * width, (i + 1) * width) for i in range(3)]
        loc = [local(xt.at[m, first], xa1.at[m], m, 0), local(xt.at[m, second], xa2.at[m], m, 1),
               local(xt.at[m, third], xo.at[m], m, 2), local(xt.at[m, own], xf.at[m], m, 3)]
        far = [to_mate(xt.at[m, first], xa1.at[n_micro + m], m, 0), to_mate(xt.at[m, second], xa2.at[n_micro + m], m, 1),
               to_mate(xt.at[m, third], xo.at[n_micro + m], m, 2), to_mate(xt.at[m, fore], xf.at[n_micro + m], m, 3)]
        return loc, far

    def out_copy(m):
        return local(obuf.at[m], so_out.at[m], m, 4)

    def bwd_exports(m):
        own, fore = [[aligned(c * h, h) for h in (half_mlp, half_w, half_qkv)] for c in (core, other)]
        loc = [local(gbuf.at[m], gy_out.at[m], m, 5), local(dz.at[m, :, own[0]], dz_out.at[m], m, 6),
               local(dres.at[m, :, own[1]], dr_out.at[m], m, 7), local(dqkv.at[m, :, own[2]], dqkv_out.at[m], m, 8),
               local(gibuf.at[m], sg_out.at[m], m, 9)]
        far = [to_mate(gbuf.at[m], gy_out.at[n_micro + m], m, 4), to_mate(dz.at[m, :, fore[0]], dz_out.at[n_micro + m], m, 5),
               to_mate(dres.at[m, :, fore[1]], dr_out.at[n_micro + m], m, 6),
               to_mate(dqkv.at[m, :, fore[2]], dqkv_out.at[n_micro + m], m, 7)]
        return loc, far

    def row(i):
        return vec_ref[i:i + 1, :].astype(F32)

    def norm(m, src, idx):
        mean = jnp.sum(src, axis=-1, keepdims=True) * (1.0 / width)
        cen = src - mean
        var = jnp.sum(cen * cen, axis=-1, keepdims=True) * (1.0 / width)
        rs = lax.rsqrt(var + 1e-5)
        stats[m, 2 * idx] = mean
        stats[m, 2 * idx + 1] = rs
        return cen * rs

    def add_vec(i, val):
        for t in range(val.shape[1] // LANES):
            vsum[i + t:i + t + 1, :] = vsum[i + t:i + t + 1, :] + val[:, LANES * t:LANES * (t + 1)]

    lane = lax.broadcasted_iota(jnp.int32, (1, LANES), 1)
    head_mask = [(lane < 64).astype(F32).astype(BF16), (lane >= 64).astype(F32).astype(BF16)]
    key_ok = lax.broadcasted_iota(jnp.int32, (TOK, KEYS), 1) < seq
    scale = 1.0 / math.sqrt(64)
    n_tile = mlp // width

    def flip_weights():
        def blocks(n, src, dst, by_row):
            def body(i, c):
                at = pl.ds(pl.multiple_of(i * KEYS, LANES), KEYS)
                if by_row:
                    dst[:, at] = src[at, :].T
                else:
                    dst[at, :] = src[:, at].T
                return c
            lax.fori_loop(0, n, body, 0)
        blocks(mlp // KEYS, w2, w2_t, True)
        blocks(mlp // KEYS, w1, w1_t, False)
        blocks(width // KEYS, wproj, wproj_t, False)
        blocks(3 * width // KEYS, wqkv, wqkv_t, False)

    def flip_acts(m, carry):
        fill = jnp.zeros((KEYS - TOK, width), BF16)
        for i, src in enumerate((a1, a2, att)):
            xt[m, i * width:(i + 1) * width, :] = jnp.concatenate([src[m], fill], axis=0).T

        def body(j, c):
            rows = pl.ds(pl.multiple_of((3 + j) * width, LANES), width)
            xt[m, rows, :] = jnp.concatenate([fact[m, :, aligned(j * width, width)], fill], axis=0).T
            return c
        lax.fori_loop(0, n_tile, body, 0)
        loc, far = fwd_exports(m)
        for c in loc + far:
            c.start()
        return carry

    def forward(m, carry):
        @pl.when(stage == 0)
        def _():
            x_load(m).wait()

        @pl.when(stage > 0)
        def _():
            fwd_copy(m).wait_recv()

        h = hbuf[m].astype(F32)
        a1[m] = (norm(m, h, 0) * row(0) + row(1)).astype(BF16)

        @pl.when((m == 0) & (stage == 0))
        def _():
            loads[0].wait()
        for j in range(3):
            cols = slice(j * width, (j + 1) * width)
            qkv[m, :TOK, cols] = (dot_nn(a1[m], wqkv[:, cols]) + row(2 + j)).astype(BF16)

        def attend(p):
            q2 = qkv[m, :TOK, aligned(p * LANES, LANES)]
            k2 = qkv[m, :, aligned(width + p * LANES, LANES)]
            v2 = qkv[m, :, aligned(2 * width + p * LANES, LANES)]
            out = None
            for e in range(2):
                s = rounded(dot_nt(q2 * head_mask[e], k2) * scale)
                s = jnp.where(key_ok, s, -1e30)
                ex = jnp.exp(s - jnp.max(s, axis=-1, keepdims=True))
                pr = ex * (1.0 / jnp.sum(ex, axis=-1, keepdims=True))
                prob[m, 2 * p + e] = pr
                o = dot_nn(pr.astype(BF16), v2 * head_mask[e])
                out = o if out is None else out + o
            att[m, :, aligned(p * LANES, LANES)] = out.astype(BF16)

        def attend_some(i, c):
            for j in range(PAIRS):
                attend(PAIRS * i + j)
            return c
        lax.fori_loop(0, heads // 2 // PAIRS, attend_some, 0)

        @pl.when((m == 0) & (stage == 0))
        def _():
            loads[1].wait()
        r = (hbuf[m].astype(F32) + dot_nn(att[m], wproj[...]) + row(5)).astype(BF16)
        res[m] = r
        a2[m] = (norm(m, r.astype(F32), 1) * row(6) + row(7)).astype(BF16)

        @pl.when((m == 0) & (stage == 0))
        def _():
            loads[2].wait()

        def expand(j, c):
            cols = aligned(j * width, width)
            z = (dot_nn(a2[m], w1[:, cols]) + bf1_ref[:, cols].astype(F32)).astype(BF16)
            zact[m, :, cols] = z
            z = z.astype(F32)
            fact[m, :, cols] = (z * (0.5 + 0.5 * lax.erf(z * math.sqrt(0.5)))).astype(BF16)
            return c
        lax.fori_loop(0, n_tile, expand, 0)

        @pl.when((m == 0) & (stage == 0))
        def _():
            loads[3].wait()
        obuf[m] = (res[m].astype(F32) + dot_nn(fact[m], w2[...]) + row(8)).astype(BF16)

        @pl.when(stage < last)
        def _():
            fwd_copy(m).start()
        out_copy(m).start()
        return carry

    def norm_back(m, src, idx, g, gain, shift_row, skip):
        xhat = (src - stats[m, 2 * idx]) * stats[m, 2 * idx + 1]
        add_vec(shift_row, jnp.sum(g, axis=0, keepdims=True))
        gx = g * xhat
        add_vec(shift_row - width // LANES, jnp.sum(gx, axis=0, keepdims=True))
        m1 = jnp.sum(g * gain, axis=-1, keepdims=True) * (1.0 / width)
        m2 = jnp.sum(gx * gain, axis=-1, keepdims=True) * (1.0 / width)
        return (skip + stats[m, 2 * idx + 1] * (g * gain - m1 - xhat * m2)).astype(BF16)

    vr = width // LANES

    def backward(m, carry):
        @pl.when(stage == last)
        def _():
            g_load(m).wait()

        @pl.when(stage < last)
        def _():
            bwd_copy(m).wait_recv()

        def contract(j, c):
            cols = aligned(j * width, width)
            ga = rounded(dot_nn(gbuf[m], w2_t[:, cols]))
            z = zact[m, :, cols].astype(F32)
            cdf = 0.5 + 0.5 * lax.erf(z * math.sqrt(0.5))
            pdf = jnp.exp(z * z * -0.5) * (1.0 / math.sqrt(2.0 * math.pi))
            dz[m, :, cols] = (ga * (cdf + z * pdf)).astype(BF16)
            return c
        lax.fori_loop(0, n_tile, contract, 0)
        g2 = rounded(dot_nn(dz[m], w1_t[...]))
        dr = norm_back(m, res[m].astype(F32), 1, g2, row(6), 7 * vr, gbuf[m].astype(F32))
        dres[m] = dr
        datt[...] = dot_nn(dr, wproj_t[...]).astype(BF16)

        def attend_back(p):
            q2 = qkv[m, :TOK, aligned(p * LANES, LANES)]
            k2 = qkv[m, :, aligned(width + p * LANES, LANES)]
            v2 = qkv[m, :, aligned(2 * width + p * LANES, LANES)]
            do2 = datt[:, aligned(p * LANES, LANES)]
            dq = dk = dv = None
            for e in range(2):
                pr = prob[m, 2 * p + e]
                qe, ke, de = q2 * head_mask[e], k2 * head_mask[e], do2 * head_mask[e]
                dp_ = rounded(dot_nt(de, v2))
                t = jnp.sum(pr * dp_, axis=-1, keepdims=True)
                ds = (pr * (dp_ - t)).astype(BF16)
                parts = dot_nn(ds, ke), dot_tn(ds, qe), dot_tn(pr.astype(BF16), de)
                dq, dk, dv = parts if dq is None else (dq + parts[0], dk + parts[1], dv + parts[2])
            dqkv[m, :, aligned(p * LANES, LANES)] = (dq * scale).astype(BF16)
            dqkv[m, :, aligned(width + p * LANES, LANES)] = (dk[:TOK] * scale).astype(BF16)
            dqkv[m, :, aligned(2 * width + p * LANES, LANES)] = dv[:TOK].astype(BF16)

        def attend_back_some(i, c):
            for j in range(PAIRS):
                attend_back(PAIRS * i + j)
            return c
        lax.fori_loop(0, heads // 2 // PAIRS, attend_back_some, 0)
        g1 = rounded(dot_nn(dqkv[m], wqkv_t[...]))
        gibuf[m] = norm_back(m, hbuf[m].astype(F32), 0, g1, row(0), vr, dres[m].astype(F32))

        @pl.when(stage > 0)
        def _():
            bwd_copy(m).start()
        loc, far = bwd_exports(m)
        for c in loc + far:
            c.start()
        return carry

    @pl.when(stage > 0)
    def _():
        for ld in loads:
            ld.wait()
        flip_weights()
    lax.fori_loop(0, n_micro, forward, 0)

    @pl.when(stage == 0)
    def _():
        flip_weights()

    @pl.when(stage < last)
    def _():
        lax.fori_loop(0, n_micro, flip_acts, 0)
    lax.fori_loop(0, n_micro, backward, 0)

    @pl.when(stage == last)
    def _():
        lax.fori_loop(0, n_micro, flip_acts, 0)

    def sums(m, carry):
        for j in range(3):
            add_vec((2 + j) * vr, jnp.sum(dqkv[m, :, j * width:(j + 1) * width].astype(F32), axis=0, keepdims=True))
        add_vec(5 * vr, jnp.sum(dres[m].astype(F32), axis=0, keepdims=True))
        add_vec(8 * vr, jnp.sum(gbuf[m].astype(F32), axis=0, keepdims=True))
        for j in range(n_tile):
            add_vec(9 * vr + j * vr, jnp.sum(dz[m, :, j * width:(j + 1) * width].astype(F32), axis=0, keepdims=True))
        return carry
    lax.fori_loop(0, n_micro, sums, 0)

    vec_loc = pltpu.make_async_copy(vsum, vec_out.at[0], vec_sem.at[0])
    vec_far = pltpu.make_async_remote_copy(vsum, vec_out.at[1], vec_sem.at[1], vec_sem.at[2],
                                           device_id={'dp': mate}, device_id_type=MESH)
    vec_loc.start()
    vec_far.start()
    for m in range(n_micro):
        @pl.when(stage < last)
        def _():
            fwd_copy(m).wait_send()

        @pl.when(stage > 0)
        def _():
            bwd_copy(m).wait_send()
        out_copy(m).wait()
        for loc, far in (fwd_exports(m), bwd_exports(m)):
            for c in loc:
                c.wait()
            for c in far:
                c.wait_send()
                c.wait_recv()
    vec_loc.wait()
    vec_far.wait_send()
    vec_far.wait_recv()


FIRST_Y = {'fc1': True, 'qkv': True, 'fc2': False, 'proj': False, 'vec': True}
ROWS = {'fc1': 768, 'qkv': 768, 'fc2': 1536, 'proj': 768, 'vec': 256}
PLUS = {'fc1': 6, 'qkv': 5, 'fc2': 3, 'proj': 2}
MINUS = {'fc1': 6, 'qkv': 4, 'fc2': 3, 'proj': 1}
WIDEST = {'fc1': 2, 'qkv': 2, 'fc2': 1, 'proj': 1}


def make_pieces():
    pieces = []
    for name in ('fc1', 'qkv', 'fc2', 'proj'):
        col = 0
        for way, tiles in ((1, PLUS[name]), (-1, MINUS[name])):
            k = -(-tiles // WIDEST[name])
            for i in range(k):
                t = tiles // k + (1 if i < tiles % k else 0)
                pieces.append((name, way, col * LANES, t * LANES))
                col += t
    return pieces + [('vec', 1, 0, LANES)]


def make_order(pieces, ny, nz, rate=51.3e3, lat=2.79, lat_y=0.3, first=5.0, ready=15.0, step=0.0736):
    heap, order, waiting, free, count = [], [], {}, {}, [0]

    def on_y(i, ph):
        return FIRST_Y[pieces[i][0]] == (ph == 1)

    def ring(i, ph):
        return ny if on_y(i, ph) else nz

    def nbytes(i, ph):
        rows = ROWS[pieces[i][0]] // ring(i, 1)
        return (rows if ph == 1 else rows // ring(i, 2)) * pieces[i][3] * 4

    def push(t, item):
        count[0] += 1
        heapq.heappush(heap, (t, count[0], item))

    def dispatch(t, key):
        queue = waiting.get(key)
        if queue and free.get(key, 0.0) <= t + 1e-9:
            typ, i, ph, k = heapq.heappop(queue)[-1]
            w = nbytes(i, ph) / rate
            free[key] = t + w
            order.append(('send', typ, i, ph, k))
            push(t + w, ('free', key))
            push(t + w + lat + (lat_y if key[0] else 0.0), ('land', (typ, i, ph, k)))

    def enqueue(t, typ, i, ph, k):
        way = pieces[i][1] * (1 if typ == 'rs' else -1)
        key = (on_y(i, ph), way)
        count[0] += 1
        heapq.heappush(waiting.setdefault(key, []), ((ph == 1 and typ == 'ag', ph == 1, -k if typ == 'rs' else 0, i), count[0], (typ, i, ph, k)))
        dispatch(t, key)

    for i in range(len(pieces)):
        push(first, ('start', i))
    seq = ready
    while heap:
        t, _, item = heapq.heappop(heap)
        if item[0] == 'free':
            dispatch(t, item[1])
        elif item[0] == 'start':
            enqueue(t, 'rs', item[1], 1, 0)
        elif item[0] == 'land':
            seq = max(seq, t) + step
            push(seq, ('done', item[1]))
        else:
            typ, i, ph, k = item[1]
            order.append(('recv', typ, i, ph, k))
            if k < ring(i, ph) - 2:
                enqueue(t, typ, i, ph, k + 1)
            elif typ == 'rs':
                enqueue(t, 'rs' if ph == 1 else 'ag', i, 2, 0)
            elif ph == 2:
                enqueue(t, 'ag', i, 1, 0)
    return order


def grad_kernel(cfg, *refs):
    ny, nz, n_img, pieces, order = cfg
    n_p = len(pieces)
    it = iter(refs)
    take = lambda n: [next(it) for _ in range(n)]
    x_in = dict(zip(('fc1', 'fc2', 'qkv', 'proj'), take(4)))
    y_in = dict(zip(('fc1', 'fc2', 'qkv', 'proj'), take(4)))
    (vec_in,) = take(1)
    out = dict(zip(('fc1', 'fc2', 'qkv', 'proj', 'vec'), take(5)))
    x_t = dict(zip(('fc1', 'fc2', 'qkv', 'proj'), take(4)))
    y_v = dict(zip(('fc1', 'fc2', 'qkv', 'proj'), take(4)))
    (vec_v,) = take(1)
    acc = dict(zip(('fc1', 'fc2', 'qkv', 'proj', 'vec'), take(5)))
    slot1, slot2 = take(n_p), take(n_p)
    ld_sem, send_sem, recv_sem, out_sem, mate_send, mate_recv = take(6)

    dp = lax.axis_index('dp')
    core = lax.rem(dp, 2)
    mate = dp + 1 - 2 * core
    py = lax.rem(lax.div(dp, 2), ny)
    pz = lax.div(dp, 2 * ny)

    def at(y, z):
        return (z * ny + y) * 2 + core

    def turn(pos, by, n):
        return lax.rem(pos + by % n, n)

    nbr = {(True, 1): at(turn(py, 1, ny), pz), (True, -1): at(turn(py, -1, ny), pz),
           (False, 1): at(py, turn(pz, 1, nz)), (False, -1): at(py, turn(pz, -1, nz))}

    names = ('fc1', 'fc2', 'qkv', 'proj')
    loads = []
    for j, name in enumerate(names):
        for s in range(n_img):
            loads.append((name, pltpu.make_async_copy(x_in[name].at[s], x_t[name].at[s], ld_sem.at[j, 0, s])))
            loads.append((name, pltpu.make_async_copy(y_in[name].at[s], y_v[name].at[s, 0:TOK, :], ld_sem.at[j, 1, s])))
    vec_load = pltpu.make_async_copy(vec_in, vec_v, ld_sem.at[4, 0, 0])
    for _, ld in loads:
        ld.start()
    vec_load.start()

    barrier = pltpu.get_barrier_semaphore()
    for dev in list(nbr.values()) + [mate]:
        pl.semaphore_signal(barrier, inc=1, device_id={'dp': dev}, device_id_type=MESH)

    for name in names:
        y_v[name][:, TOK:, :] = jnp.zeros((n_img, KEYS - TOK, y_v[name].shape[2]), BF16)
    pl.semaphore_wait(barrier, 5)

    def ring(i, ph):
        return ny if FIRST_Y[pieces[i][0]] == (ph == 1) else nz

    def place(i, ph):
        return py if FIRST_Y[pieces[i][0]] == (ph == 1) else pz

    def rows1(i, by):
        size = ROWS[pieces[i][0]] // ring(i, 1)
        return pl.ds(pl.multiple_of(turn(place(i, 1), by, ring(i, 1)) * size, 8), size)

    def rows2(i, by):
        big = ROWS[pieces[i][0]] // ring(i, 1)
        size = big // ring(i, 2)
        return pl.ds(pl.multiple_of(place(i, 1) * big + turn(place(i, 2), by, ring(i, 2)) * size, 8), size)

    def view(i, ph, by):
        name, _, col, cols = pieces[i]
        rows = rows1(i, by) if ph == 1 else rows2(i, by)
        return acc[name].at[rows, col:col + cols]

    steps = {}
    for _, typ, i, ph, k in order:
        steps.setdefault((typ, i, ph, k), len(steps))

    def landing(i, ph, k):
        n = ring(i, ph)
        return n - 3 - k if k <= n - 3 else n - 1

    def sent(group, i):
        slots = ((slot1, slot2)[group % 2])[i]
        part = slots.at[0:slots.shape[0] - 1]
        pltpu.make_async_copy(part, part, send_sem.at[group * n_p + i]).wait()

    def copy(typ, i, ph, k):
        way = pieces[i][1] * (1 if typ == 'rs' else -1)
        group = ((0 if typ == 'rs' else 2) + ph - 1) * n_p + i
        slots = (slot1 if ph == 1 else slot2)[i]
        if typ == 'rs':
            src, dst = view(i, ph, -way * (1 + k)), slots.at[k]
        else:
            src = slots.at[landing(i, ph, k - 1)] if k else view(i, ph, 0)
            dst = slots.at[landing(i, ph, k)]
        return pltpu.make_async_remote_copy(src, dst, send_sem.at[group], recv_sem.at[steps[typ, i, ph, k]],
                                            device_id={'dp': nbr[FIRST_Y[pieces[i][0]] == (ph == 1), way]}, device_id_type=MESH)

    def home(i, rows):
        name, _, col, cols = pieces[i]
        if name == 'vec':
            return out[name].at[rows, :]
        if name == 'fc2':
            return out[name].at[pl.ds(pl.multiple_of(core * ROWS[name] + rows.start, 8), rows.size), col:col + cols]
        half = (PLUS[name] + MINUS[name]) * LANES
        return out[name].at[rows, aligned(core * half + col, cols)]

    def deliver(i, src, by):
        name = pieces[i][0]
        dst = home(i, rows1(i, by))
        pltpu.make_async_copy(src, dst, out_sem.at[i]).start()
        if name != 'vec':
            pltpu.make_async_remote_copy(src, dst, mate_send.at[i], mate_recv.at[i],
                                         device_id={'dp': mate}, device_id_type=MESH).start()

    def multiply(k, c, name):
        i = next(j for j in range(n_p) if pieces[j][0] == name)
        size = ROWS[name] // ring(i, 1)
        split = PLUS[name] * LANES
        for way, cols in ((1, slice(0, split)), (-1, slice(split, split + MINUS[name] * LANES))):
            idx = lax.rem(place(i, 1) + (2 * ring(i, 1) - way) - way * k, ring(i, 1))
            rows = pl.ds(pl.multiple_of(idx * size, 8), size)
            acc[name][rows, cols] = sum(dot_nn(x_t[name][s, rows, :], y_v[name][s, :, cols]) for s in range(n_img))
        return c

    n_first = next(j for j, o in enumerate(order) if o[0] == 'recv')
    begin, todo = order[:n_first], order[n_first:]
    for name in ('vec',) + names:
        if name == 'vec':
            vec_load.wait()
            acc['vec'][...] = vec_v[0] + vec_v[1]
        else:
            for nm, ld in loads:
                if nm == name:
                    ld.wait()
            multiply(0, 0, name)
        for o in begin:
            if pieces[o[2]][0] == name:
                copy(*o[1:]).start()
    for name in names:
        i = next(j for j in range(n_p) if pieces[j][0] == name)
        lax.fori_loop(1, ring(i, 1), functools.partial(multiply, name=name), 0)

    for what, typ, i, ph, k in todo:
        if what == 'send':
            copy(typ, i, ph, k).start()
            continue
        copy(typ, i, ph, k).wait_recv()
        way = pieces[i][1] * (1 if typ == 'rs' else -1)
        if typ == 'rs':
            dst = view(i, ph, -way * (2 + k))
            dst[...] = dst[...] + (slot1 if ph == 1 else slot2)[i][k]
        elif ph == 1:
            deliver(i, slot1[i].at[landing(i, 1, k)], -way * (1 + k))
        elif k == ring(i, 2) - 2:
            sent(1, i)
            for j in range(ring(i, 2) - 1):
                dst = view(i, 2, -way * (1 + j))
                dst[...] = slot2[i][landing(i, 2, j)]
            deliver(i, view(i, 1, 0), 0)

    for i in range(n_p):
        name, _, col, cols = pieces[i]
        for group in (0, 2, 3):
            sent(group, i)
        whole = acc[name].at[:, col:col + cols]
        pltpu.make_async_copy(whole, whole, out_sem.at[i]).wait()
        if name != 'vec':
            pltpu.make_async_copy(whole, whole, mate_send.at[i]).wait()
            pltpu.make_async_copy(whole, whole, mate_recv.at[i]).wait()


def solution(mesh):
    stages = mesh.shape['pp']
    n_dp = mesh.shape['dp']
    ny = 4 if n_dp == 64 else 2
    nz = n_dp // (2 * ny)
    act_spec = P(None, 'dp')
    stage_spec = P('pp')
    out_act_spec = P('pp', None, 'dp')
    pieces = make_pieces()
    order = make_order(pieces, ny, nz)

    def per_device(x_in, grad_out, vectors, w_qkv, w_proj, w_fc1, b_fc1, w_fc2):
        n_micro, _, seq, width = x_in.shape
        mlp = w_fc1.shape[2]
        heads = w_proj.shape[1]
        pad = ((0, 0), (0, TOK - seq), (0, 0))
        x_p = jnp.pad(x_in.reshape(n_micro, seq, width), pad)
        go_p = jnp.pad(grad_out.reshape(n_micro, seq, width), pad)
        hbm, vmem = pl.BlockSpec(memory_space=pl.ANY), pl.BlockSpec(memory_space=pltpu.VMEM)
        n_img = 2 * n_micro
        act = lambda n, w: jax.ShapeDtypeStruct((n, TOK, w), BF16)
        flat = lambda f: jax.ShapeDtypeStruct((n_img, f, KEYS), BF16)
        dma, vm = pltpu.SemaphoreType.DMA, pltpu.VMEM
        outs = pl.pallas_call(
            functools.partial(pipeline_kernel, (seq, stages, n_micro)),
            name='pipeline',
            out_shape=[act(n_micro, width), act(n_micro, width), flat(width), flat(width), flat(width), flat(mlp // 2),
                       act(n_img, 3 * width // 2), act(n_img, mlp // 2), act(n_img, width // 2),
                       act(n_img, width), jax.ShapeDtypeStruct((2, 256, LANES), F32)],
            in_specs=[hbm, hbm, vmem, vmem, hbm, hbm, hbm, hbm],
            out_specs=[hbm] * 11,
            scratch_shapes=[
                vm((width, 3 * width), BF16), vm((width, width), BF16), vm((width, mlp), BF16), vm((mlp, width), BF16),
                vm((3 * width, width), BF16), vm((width, width), BF16), vm((mlp, width), BF16), vm((width, mlp), BF16),
                vm((n_micro, 3 * width + mlp, KEYS), BF16),
                vm((n_micro, TOK, width), BF16), vm((n_micro, TOK, width), BF16), vm((n_micro, TOK, width), BF16),
                vm((n_micro, TOK, width), BF16), vm((n_micro, TOK, width), BF16), vm((n_micro, KEYS, 3 * width), BF16),
                vm((n_micro, TOK, width), BF16), vm((n_micro, TOK, width), BF16), vm((n_micro, TOK, width), BF16),
                vm((n_micro, TOK, mlp), BF16), vm((n_micro, TOK, mlp), BF16), vm((n_micro, heads, TOK, KEYS), F32),
                vm((n_micro, 4, TOK, 1), F32), vm((n_micro, TOK, mlp), BF16), vm((n_micro, TOK, width), BF16),
                vm((TOK, width), BF16), vm((n_micro, TOK, 3 * width), BF16), vm((256, LANES), F32),
                dma((4,)), dma((2 * n_micro,)), dma((2 * n_micro,)), dma((2 * n_micro,)), dma((n_micro, 10)),
                dma((n_micro, 8)), dma((n_micro, 8)), dma((3,)),
            ],
            compiler_params=pltpu.CompilerParams(collective_id=0, has_side_effects=True, vmem_limit_bytes=67043328),
        )(x_p, go_p, vectors[0], b_fc1, w_qkv[0], w_proj[0].reshape(width, width), w_fc1[0], w_fc2[0])
        so, sg, xa1, xa2, xo, xf, dqkv, dz, dr, gy, vec = outs

        half = {'fc1': mlp // 2, 'fc2': width, 'qkv': 3 * width // 2, 'proj': width // 2}
        feats = {'fc1': width, 'fc2': mlp // 2, 'qkv': width, 'proj': width}
        names = ('fc1', 'fc2', 'qkv', 'proj')
        f32 = lambda *s: jax.ShapeDtypeStruct(s, F32)
        slots = [[], []]
        for name, _, _, cols in pieces:
            n1, n2 = (ny, nz) if FIRST_Y[name] else (nz, ny)
            slots[0].append(vm((n1, ROWS[name] // n1, cols), F32))
            slots[1].append(vm((n2, ROWS[name] // (n1 * n2), cols), F32))
        grads = pl.pallas_call(
            functools.partial(grad_kernel, (ny, nz, n_img, pieces, order)),
            name='gradients',
            out_shape=[f32(width, mlp), f32(mlp, width), f32(width, 3 * width), f32(width, width), f32(256, LANES)],
            in_specs=[hbm] * 9,
            out_specs=[hbm] * 5,
            scratch_shapes=(
                [vm((n_img, feats[n], KEYS), BF16) for n in names] + [vm((n_img, KEYS, half[n]), BF16) for n in names] + [vm((2, 256, LANES), F32)]
                + [vm((feats[n], half[n]), F32) for n in names] + [vm((256, LANES), F32)] + slots[0] + slots[1]
                + [dma((5, 2, n_img)), dma((4 * len(pieces),)), dma((len([o for o in order if o[0] == 'send']),)),
                   dma((len(pieces),)), dma((len(pieces),)), dma((len(pieces),))]),
            compiler_params=pltpu.CompilerParams(collective_id=1, has_side_effects=True, vmem_limit_bytes=63 * 1024 * 1024),
        )(xa2, xf, xa1, xo, dz, gy, dqkv, dr, vec)
        g_fc1, g_fc2, g_qkv, g_proj, g_vec = grads
        n_vec = vectors.shape[1] * width // LANES
        g_vectors = g_vec[:n_vec].reshape(1, vectors.shape[1], width)
        g_bfc1 = g_vec[n_vec:n_vec + mlp // LANES].reshape(1, mlp)
        return (so[:, :seq].reshape(1, n_micro, 1, seq, width), sg[:, :seq].reshape(1, n_micro, 1, seq, width), g_vectors,
                g_qkv[None], g_proj.reshape(1, heads, width // heads, width), g_fc1[None], g_bfc1, g_fc2[None])

    return jax.shard_map(per_device, mesh=mesh, in_specs=(act_spec, act_spec) + (stage_spec,) * 6,
                         out_specs=(out_act_spec, out_act_spec) + (stage_spec,) * 6, check_vma=False)
```

profile of v0, /device:TPU:1, one launch (start us, length us, event | category | flops | bytes accessed | tf_op | source)
XLA Modules:
  0.0 353.6 jit_solution(775273837202553553)
XLA Ops:
  0.6 1.1 copy.29
  1.8 0.9 pad.7.x_in
  2.6 1.1 copy.28
  3.8 0.9 pad.8.go_in
  4.7 138.7 %pipeline.1 = (bf16[2,208,768]{2,1,0:T(8,128)(2,1)}, bf16[2,208,768]{2,1,0:T(8,128)(2,1)}, bf16[4,768,256]{2,1,0:T(8,128)(2,1)}, bf16[4,768,256]{2,1,0:T(8,128)(...) custom-call(bf16[2,208,768]{2,1,0:T(8,128)(2,1)} %pad.7.x_in, ...), custom_call_target="tpu_custom_call" | custom-call | tf_op jit(solution)/shard_map/pipeline/pallas_call | solution.py:647
  143.4 1.3 slice_bitcast_fusion
  144.7 1.3 copy.24
  146.0 1.3 copy.23
  147.3 183.8 %gradients.1 = (f32[768,3072]{1,0:T(8,128)}, f32[3072,768]{1,0:T(8,128)}, f32[768,2304]{1,0:T(8,128)}, f32[768,768]{1,0:T(8,128)}, f32[256,128]{1,0:T(8,128)}) custom-call(bf16[4,768,256]{2,1,0:T(8,128)(2,1)} %get-tuple-element.26.refs_0_, bf16[4,1536,256]{2,1,0:T(8,128)(2,1)} %get-tuple-element.27.refs_1_, bf16[4,768,256]{2,1,0:T(8,128)(2,1)} %get-tuple-element.28.refs_2_, ...), custom_call_target="tpu_custom_call" | custom-call | tf_op jit(solution)/shard_map/gradients/pallas_call | solution.py:681
  331.1 1.3 slice.15
  332.4 0.8 slice.14
  333.2 0.6 reshape.44
  333.8 0.0 copy-start.1
  333.8 0.0 copy-start
  333.8 7.2 %copy.34 = f32[1,768,2304]{2,1,0:T(8,128)} copy(f32[1,768,2304]{2,1,0:T(8,128)} %bitcast.24) | data formatting | bytes 14155776
  341.0 0.0 copy-done.1
  341.0 0.0 slice-start
  341.0 1.4 copy.35
  342.5 1.2 copy-done
  343.7 0.0 slice-start.1
  343.7 0.0 slice-start.2
  343.7 4.8 %copy.36 = f32[1,768,3072]{2,1,0:T(8,128)} copy(f32[1,768,3072]{2,1,0:T(8,128)S(1)} %bitcast.23) | data formatting | bytes 18874368
  348.4 0.0 slice-done
  348.4 1.2 slice-done.1
  349.6 0.2 slice-done.2
  349.8 3.7 %copy.37 = f32[1,3072,768]{2,1,0:T(8,128)} copy(f32[1,3072,768]{2,1,0:T(8,128)S(1)} %bitcast.22) | data formatting | bytes 18874368
  (1 shorter events, 0.0 us)
Async XLA Ops:
  333.8 7.2 %copy-start.1 = (f32[768,768]{1,0:T(8,128)S(1)}, f32[768,768]{1,0:T(8,128)}, u32[]{:S(2)}) copy-start(f32[768,768]{1,0:T(8,128)} %get-tuple-element.37) | copy-start | bytes 7077892
  333.8 9.8 %copy-start = (f32[768,3072]{1,0:T(8,128)S(1)}, f32[768,3072]{1,0:T(8,128)}, u32[]{:S(2)}) copy-start(f32[768,3072]{1,0:T(8,128)} %get-tuple-element.38) | copy-start | bytes 28311556
  341.0 7.4 %slice-start = ((s8[9437184]{0:T(1024)(128)(4,1)}), s8[4194304]{0:T(1024)(128)(4,1)S(1)}, s32[]{:S(2)}) async-start(s8[9437184]{0:T(1024)(128)(4,1)} %bitcast.20), calls=%async_computation | async-start | bytes 8388608
  343.7 6.0 %slice-start.1 = ((s8[9437184]{0:T(1024)(128)(4,1)}), s8[4194304]{0:T(1024)(128)(4,1)S(1)}, s32[]{:S(2)}) async-start(s8[9437184]{0:T(1024)(128)(4,1)} %bitcast.20), calls=%async_computation.1 | async-start | bytes 8388608
  343.7 6.2 %slice-start.2 = ((s8[9437184]{0:T(1024)(128)(4,1)}), s8[1048576]{0:T(1024)(128)(4,1)S(1)}, s32[]{:S(2)}) async-start(s8[9437184]{0:T(1024)(128)(4,1)} %bitcast.20), calls=%async_computation.2 | async-start | bytes 2097152
where the time goes:
time: 354 us
  Pallas kernels  323 us (91%)
  local copies, waits for them, and re-layouts  30.4 us (9%)
    pallas_call x1, Pallas kernels, per_device(): pl.pallas_call(functools.partial(grad_kernel, (ny, nz, n_img, pieces, ord...  184 us
    pallas_call x1, Pallas kernels, per_device(): pl.pallas_call(functools.partial(pipeline_kernel, (seq, stages, n_micro))...  139 us
    unnamed x18, local copies, waits for them, and re-layouts  24.6 us

commit v1 on v0

v1 whole, which is shorter than its diff:
```python
import functools
import heapq
import math
import jax
import jax.numpy as jnp
from jax import lax
from jax.experimental import pallas as pl
from jax.experimental.pallas import tpu as pltpu
from jax.sharding import PartitionSpec as P

MESH = pl.DeviceIdType.MESH
F32 = jnp.float32
BF16 = jnp.bfloat16
TOK = 208
KEYS = 256
SENT = 200
LANES = 128
HEAD = 64
WIDE = 512
SPLIT = 112
SHIFT = 6200


def dot_nn(a, b):
    return jnp.dot(a, b, preferred_element_type=F32)


def dot_nt(a, b):
    return lax.dot_general(a, b, (((1,), (1,)), ((), ())), preferred_element_type=F32)


def rounded(x):
    return x.astype(BF16).astype(F32)


def aligned(start, size):
    return pl.ds(pl.multiple_of(start, LANES), size)


def row_sum(x):
    return jnp.sum(x, axis=-1, keepdims=True)


def col_sum(x):
    return jnp.sum(x.astype(F32), axis=0, keepdims=True)


def loop(n, body):
    def step(i, c):
        body(i)
        return c
    lax.fori_loop(0, n, step, 0)


def tiles(total):
    wide = total - total % WIDE
    out = [(slice(0, TOK), slice(c, c + WIDE)) for c in range(0, wide, WIDE)]
    if wide < total:
        out += [(rows, slice(wide, total)) for rows in (slice(0, SPLIT), slice(SPLIT, TOK))]
    return out


def pipeline_kernel(cfg, x_in, go_in, vec_ref, bf1_ref, wqkv_in, wproj_in, w1_in, w2_in,
                    so_out, sg_out, xa1, xa2, xo, xf, dqkv_out, dz_out, dr_out, gy_out, vec_out,
                    wqkv, wproj, w1, w2, wqkv_t, wproj_t, w1_t, w2_t, xt, x_raw, g_raw,
                    hbuf, gbuf, obuf, gibuf, a1, qkv, att, res, a2, zact, fact, prob, prob16, stats,
                    dz, dres, datt, gtmp, dqkv, raw16, ds16, vsum,
                    w_sem, in_sem, send_sem, recv_sem, loc_sem, psend_sem, precv_sem, vec_sem):
    seq, stages, n_micro = cfg
    width = wproj.shape[0]
    mlp = w1.shape[1]
    pairs = width // LANES
    half_qkv, half_mlp, half_w = 3 * width // 2, mlp // 2, width // 2
    dp = lax.axis_index('dp')
    stage = lax.axis_index('pp')
    core = lax.rem(dp, 2)
    mate = dp + 1 - 2 * core
    cores = (core, 1 - core)
    last = stages - 1
    nxt = lax.rem(stage + 1, stages)
    prv = lax.rem(stage + last, stages)
    at_first, at_last = pl.when(stage == 0), pl.when(stage == last)
    past_first, before_last = pl.when(stage > 0), pl.when(stage < last)
    remote = functools.partial(pltpu.make_async_remote_copy, device_id_type=MESH)

    loads = [pltpu.make_async_copy(src, dst, w_sem.at[i])
             for i, (src, dst) in enumerate(((wqkv_in, wqkv), (wproj_in, wproj), (w1_in, w1), (w2_in, w2)))]
    x_load = pltpu.make_async_copy(x_in, x_raw, in_sem.at[0])
    g_load = pltpu.make_async_copy(go_in, g_raw, in_sem.at[1])

    def split(raw, dst):
        for m in range(n_micro):
            dst[m, :seq] = raw[:, m, :]
            dst[m, seq:] = jnp.zeros((TOK - seq, width), BF16)

    at_first(x_load.start)
    for ld in loads:
        ld.start()
    at_last(g_load.start)

    barrier = pltpu.get_barrier_semaphore()
    for dev in ({'pp': nxt}, {'pp': prv}, {'dp': mate}):
        pl.semaphore_signal(barrier, device_id=dev, device_id_type=MESH)
    qkv[:, TOK:, :] = jnp.zeros((n_micro, KEYS - TOK, 3 * width), BF16)
    datt[TOK:, :] = jnp.zeros((KEYS - TOK, width), BF16)
    for buf in (hbuf, gbuf):
        buf[:, SENT:, :] = jnp.zeros((n_micro, TOK - SENT, width), BF16)
    vsum[...] = jnp.zeros(vsum.shape, F32)
    pl.semaphore_wait(barrier, 3)

    @pl.when((stage == 0) & (core == 1))
    def _():
        pl.delay(SHIFT)

    def fwd_copy(m):
        return remote(obuf.at[m, :SENT], hbuf.at[m, :SENT], send_sem.at[m], recv_sem.at[m], device_id={'pp': nxt})

    def bwd_copy(m):
        return remote(gibuf.at[m, :SENT], gbuf.at[m, :SENT], send_sem.at[n_micro + m], recv_sem.at[n_micro + m], device_id={'pp': prv})

    def local(src, dst, m, i):
        return pltpu.make_async_copy(src, dst, loc_sem.at[m, i])

    def exports(m, first, whole, halved):
        loc, far = [], []
        for i, (src, dst) in enumerate(whole + halved, first):
            for c, out in zip(cores, (loc, far)):
                part = src(m, c) if callable(src) else src.at[m]
                out.append(local(part, dst.at[m], m, i) if out is loc else
                           remote(part, dst.at[n_micro + m], psend_sem.at[m, i], precv_sem.at[m, i], device_id={'dp': mate}))
        return loc, far

    def xt_rows(i):
        return lambda m, c: xt.at[m, i * width:(i + 1) * width]

    def fwd_exports(m):
        return exports(m, 0, [(xt_rows(i), dst) for i, dst in enumerate((xa1, xa2, xo))],
                       [(lambda m, c: xt.at[m, pl.ds(pl.multiple_of(3 * width + c * half_mlp, LANES), half_mlp)], xf)])

    def half_of(ref, size):
        return lambda m, c: ref.at[m, :, aligned(c * size, size)]

    def bwd_exports(m):
        return exports(m, 4, [(gbuf, gy_out)], [(half_of(dz, half_mlp), dz_out), (half_of(dres, half_w), dr_out),
                                                (half_of(dqkv, half_qkv), dqkv_out)])

    def out_copies(m):
        return local(obuf.at[m], so_out.at[m], m, 8), local(gibuf.at[m], sg_out.at[m], m, 9)

    def row(i):
        return vec_ref[i:i + 1, :].astype(F32)

    bias_qkv = jnp.concatenate([row(i) for i in (2, 3, 4)], axis=1)

    def norm(m, src, idx):
        mean = row_sum(src) * (1.0 / width)
        cen = src - mean
        rs = lax.rsqrt(row_sum(cen * cen) * (1.0 / width) + 1e-5)
        stats[m, 2 * idx] = mean
        stats[m, 2 * idx + 1] = rs
        return cen * rs

    def add_vec(i, val):
        for t in range(val.shape[1] // LANES):
            at = slice(i * pairs + t, i * pairs + t + 1)
            vsum[at, :] = vsum[at, :] + val[:, LANES * t:LANES * (t + 1)]

    lane = lax.broadcasted_iota(jnp.int32, (1, LANES), 1)
    head_mask = [ok.astype(F32).astype(BF16) for ok in (lane < HEAD, lane >= HEAD)]
    key_ok = lax.broadcasted_iota(jnp.int32, (TOK, KEYS), 1) < seq
    scale = 1.0 / math.sqrt(HEAD)
    n_tile = mlp // width

    def flip_weights():
        for src, dst in ((w2, w2_t), (w1, w1_t), (wproj, wproj_t), (wqkv, wqkv_t)):
            by_row = src.shape[0] > src.shape[1]

            def body(i, src=src, dst=dst, by_row=by_row):
                at = aligned(i * KEYS, KEYS)
                if by_row:
                    dst[:, at] = src[at, :].T
                else:
                    dst[at, :] = src[:, at].T
            loop(max(src.shape) // KEYS, body)

    def flip_acts(m):
        fill = jnp.zeros((KEYS - TOK, width), BF16)
        for i, src in enumerate((a1, a2, att)):
            xt[m, i * width:(i + 1) * width, :] = jnp.concatenate([src[m], fill], axis=0).T

        def body(j):
            rows = pl.ds(pl.multiple_of((3 + j) * width, LANES), width)
            xt[m, rows, :] = jnp.concatenate([fact[m, :, aligned(j * width, width)], fill], axis=0).T
        loop(n_tile, body)
        for c in sum(fwd_exports(m), []):
            c.start()

    def forward(m):
        @past_first
        def _():
            fwd_copy(m).wait_recv()

        def need(i):
            pl.when((m == 0) & (stage == 0))(loads[i].wait)

        a1[m] = (norm(m, hbuf[m].astype(F32), 0) * row(0) + row(1)).astype(BF16)
        need(0)
        for rows, cols in tiles(3 * width):
            qkv[m, rows, cols] = (dot_nn(a1[m, rows], wqkv[:, cols]) + bias_qkv[:, cols]).astype(BF16)

        def scores(p):
            q2 = qkv[m, :TOK, p * LANES:(p + 1) * LANES]
            k2 = qkv[m, :, width + p * LANES:width + (p + 1) * LANES]
            for e, mask in enumerate(head_mask):
                raw16[p % 2, e] = (dot_nt(q2 * mask, k2) * scale).astype(BF16)

        def soft(p):
            for e in range(2):
                s = jnp.where(key_ok, raw16[p % 2, e].astype(F32), -1e30)
                ex = jnp.exp(s - jnp.max(s, axis=-1, keepdims=True))
                pr = ex * (1.0 / row_sum(ex))
                prob[m, 2 * p + e] = pr
                prob16[m, 2 * p + e] = pr.astype(BF16)

        def values(p):
            v2 = qkv[m, :, 2 * width + p * LANES:2 * width + (p + 1) * LANES]
            o = [dot_nn(prob16[m, 2 * p + e], v2 * mask) for e, mask in enumerate(head_mask)]
            att[m, :, p * LANES:(p + 1) * LANES] = sum(o).astype(BF16)

        staggered(pairs, (scores, soft, values))
        need(1)
        for rows, cols in tiles(width):
            res[m, rows, cols] = (hbuf[m, rows, cols].astype(F32) + dot_nn(att[m, rows], wproj[:, cols])
                                  + row(5)[:, cols]).astype(BF16)
        a2[m] = (norm(m, res[m].astype(F32), 1) * row(6) + row(7)).astype(BF16)
        need(2)
        for rows, cols in tiles(mlp):
            z = (dot_nn(a2[m, rows], w1[:, cols]) + bf1_ref[:, cols].astype(F32)).astype(BF16)
            zact[m, rows, cols] = z
            z = z.astype(F32)
            fact[m, rows, cols] = (z * (0.5 + 0.5 * lax.erf(z * math.sqrt(0.5)))).astype(BF16)
        need(3)
        for rows, cols in tiles(width):
            obuf[m, rows, cols] = (res[m, rows, cols].astype(F32) + dot_nn(fact[m, rows], w2[:, cols])
                                   + row(8)[:, cols]).astype(BF16)

        @before_last
        def _():
            fwd_copy(m).start()
        out_copies(m)[0].start()

    def norm_back(m, src, idx, gain, vec_row, skip):
        rs = stats[m, 2 * idx + 1]
        xhat = (src - stats[m, 2 * idx]) * rs
        g = gtmp[...].astype(F32)
        gx = g * xhat
        add_vec(vec_row, col_sum(gx))
        add_vec(vec_row + 1, col_sum(g))
        m1 = row_sum(g * gain) * (1.0 / width)
        m2 = row_sum(gx * gain) * (1.0 / width)
        return (skip + rs * (g * gain - m1 - xhat * m2)).astype(BF16)

    def backward(m):
        @before_last
        def _():
            bwd_copy(m).wait_recv()

        for rows, cols in tiles(mlp):
            ga = rounded(dot_nn(gbuf[m, rows], w2_t[:, cols]))
            z = zact[m, rows, cols].astype(F32)
            cdf = 0.5 + 0.5 * lax.erf(z * math.sqrt(0.5))
            pdf_z = jnp.exp2(z * z * (-0.5 * math.log2(math.e))) * (z * (1.0 / math.sqrt(2.0 * math.pi)))
            dz[m, rows, cols] = (ga * (cdf + pdf_z)).astype(BF16)
        for rows, cols in tiles(width):
            gtmp[rows, cols] = dot_nn(dz[m, rows], w1_t[:, cols]).astype(BF16)
        dres[m] = norm_back(m, res[m].astype(F32), 1, row(6), 6, gbuf[m].astype(F32))
        for rows, cols in tiles(width):
            datt[rows, cols] = dot_nn(dres[m, rows], wproj_t[:, cols]).astype(BF16)

        def dprobs(p):
            do2 = datt[:TOK, p * LANES:(p + 1) * LANES]
            v2 = qkv[m, :, 2 * width + p * LANES:2 * width + (p + 1) * LANES]
            for e, mask in enumerate(head_mask):
                raw16[p % 2, e] = dot_nt(do2 * mask, v2).astype(BF16)

        def dscores(p):
            for e in range(2):
                pr, d = prob[m, 2 * p + e], raw16[p % 2, e].astype(F32)
                ds16[p % 2, e] = (pr * (d - row_sum(pr * d))).astype(BF16)

        def dheads(p):
            q_t = qkv[m, :, p * LANES:(p + 1) * LANES].T
            k2 = qkv[m, :, width + p * LANES:width + (p + 1) * LANES]
            do_t = datt[:, p * LANES:(p + 1) * LANES].T
            dq = sum(dot_nn(ds16[p % 2, e], k2 * mask) for e, mask in enumerate(head_mask)) * scale
            dk, dv = [jnp.concatenate([dot_nn(lhs[HEAD * e:HEAD * (e + 1), :TOK], rhs(e)) for e in range(2)], axis=0)
                      for lhs, rhs in ((q_t, lambda e: ds16[p % 2, e]), (do_t, lambda e: prob16[m, 2 * p + e]))]
            for i, val in enumerate((dq.astype(BF16), (dk * scale).astype(BF16).T[:TOK], dv.astype(BF16).T[:TOK])):
                dqkv[m, :, i * width + p * LANES:i * width + (p + 1) * LANES] = val

        staggered(pairs, (dprobs, dscores, dheads))
        for rows, cols in tiles(width):
            gtmp[rows, cols] = dot_nn(dqkv[m, rows], wqkv_t[:, cols]).astype(BF16)
        gibuf[m] = norm_back(m, hbuf[m].astype(F32), 0, row(0), 0, dres[m].astype(F32))

        @past_first
        def _():
            bwd_copy(m).start()
        for c in sum(bwd_exports(m), [out_copies(m)[1]]):
            c.start()

    @at_first
    def _():
        x_load.wait()
        split(x_raw, hbuf)

    @at_last
    def _():
        g_load.wait()
        split(g_raw, gbuf)

    @past_first
    def _():
        for ld in loads:
            ld.wait()
        flip_weights()
    loop(n_micro, forward)
    at_first(flip_weights)

    @before_last
    def _():
        loop(n_micro, flip_acts)
    loop(n_micro, backward)

    @at_last
    def _():
        loop(n_micro, flip_acts)

    def sums(m):
        for j in range(3):
            add_vec(2 + j, col_sum(dqkv[m, :, j * width:(j + 1) * width]))
        add_vec(5, col_sum(dres[m]))
        add_vec(8, col_sum(gbuf[m]))
        for j in range(n_tile):
            add_vec(9 + j, col_sum(dz[m, :, j * width:(j + 1) * width]))
    loop(n_micro, sums)

    vec_loc = pltpu.make_async_copy(vsum, vec_out.at[0], vec_sem.at[0])
    vec_far = remote(vsum, vec_out.at[1], vec_sem.at[1], vec_sem.at[2], device_id={'dp': mate})
    vec_loc.start()
    vec_far.start()
    for m in range(n_micro):
        before_last(fwd_copy(m).wait_send)
        past_first(bwd_copy(m).wait_send)
        for c in out_copies(m):
            c.wait()
        for loc, far in (fwd_exports(m), bwd_exports(m)):
            for c in loc + far:
                c.wait()
    vec_loc.wait()
    vec_far.wait()


def staggered(n, phases):
    for i in range(n + len(phases) - 1):
        for d, phase in reversed(list(enumerate(phases))):
            if 0 <= i - d < n:
                phase(i - d)


WEIGHTS = ('fc1', 'fc2', 'qkv', 'proj')
PIECE_ORDER = ('fc1', 'qkv', 'fc2', 'proj')
FIRST_Y = {'fc1': True, 'qkv': True, 'fc2': False, 'proj': False, 'vec': True}
ROWS = {'fc1': 768, 'qkv': 768, 'fc2': 1536, 'proj': 768, 'vec': 256}
PLUS = {'fc1': 6, 'qkv': 5, 'fc2': 3, 'proj': 2}
MINUS = {'fc1': 6, 'qkv': 4, 'fc2': 3, 'proj': 1}
WIDEST = {'fc1': 2, 'qkv': 2, 'fc2': 1, 'proj': 1}


def make_pieces():
    pieces = []
    for name in PIECE_ORDER:
        col = 0
        for way, tiles in ((1, PLUS[name]), (-1, MINUS[name])):
            k = -(-tiles // WIDEST[name])
            for i in range(k):
                t = tiles // k + (1 if i < tiles % k else 0)
                pieces.append((name, way, col * LANES, t * LANES))
                col += t
    return pieces + [('vec', 1, 0, LANES)]


def make_order(pieces, ny, nz, rate=51.3e3, lat=2.79, lat_y=0.3, first=5.0, ready=15.0, step=0.0736):
    heap, order, waiting, free, count = [], [], {}, {}, [0]

    def on_y(i, ph):
        return FIRST_Y[pieces[i][0]] == (ph == 1)

    def ring(i, ph):
        return ny if on_y(i, ph) else nz

    def nbytes(i, ph):
        rows = ROWS[pieces[i][0]] // ring(i, 1)
        return (rows if ph == 1 else rows // ring(i, 2)) * pieces[i][3] * 4

    def push(t, item):
        count[0] += 1
        heapq.heappush(heap, (t, count[0], item))

    def dispatch(t, key):
        queue = waiting.get(key)
        if queue and free.get(key, 0.0) <= t + 1e-9:
            typ, i, ph, k = heapq.heappop(queue)[-1]
            w = nbytes(i, ph) / rate
            free[key] = t + w
            order.append(('send', typ, i, ph, k))
            push(t + w, ('free', key))
            push(t + w + lat + (lat_y if key[0] else 0.0), ('land', (typ, i, ph, k)))

    def enqueue(t, typ, i, ph, k):
        way = pieces[i][1] * (1 if typ == 'rs' else -1)
        key = (on_y(i, ph), way)
        count[0] += 1
        heapq.heappush(waiting.setdefault(key, []), ((ph == 1 and typ == 'ag', ph == 1, -k if typ == 'rs' else 0, i), count[0], (typ, i, ph, k)))
        dispatch(t, key)

    for i in range(len(pieces)):
        push(first, ('start', i))
    seq = ready
    while heap:
        t, _, item = heapq.heappop(heap)
        if item[0] == 'free':
            dispatch(t, item[1])
        elif item[0] == 'start':
            enqueue(t, 'rs', item[1], 1, 0)
        elif item[0] == 'land':
            seq = max(seq, t) + step
            push(seq, ('done', item[1]))
        else:
            typ, i, ph, k = item[1]
            order.append(('recv', typ, i, ph, k))
            if k < ring(i, ph) - 2:
                enqueue(t, typ, i, ph, k + 1)
            elif typ == 'rs':
                enqueue(t, 'rs' if ph == 1 else 'ag', i, 2, 0)
            elif ph == 2:
                enqueue(t, 'ag', i, 1, 0)
    return order


def grad_kernel(cfg, *refs):
    ny, nz, n_img, pieces, order = cfg
    n_p = len(pieces)
    it = iter(refs)
    take = lambda n: [next(it) for _ in range(n)]
    names = WEIGHTS
    each = lambda: dict(zip(names, take(len(names))))
    x_in, y_in = each(), each()
    vec_in = next(it)
    acc = each()
    acc['vec'] = next(it)
    mated = each()
    x_t, y_v = each(), each()
    vec_v = next(it)
    slot1, slot2 = take(n_p), take(n_p)
    ld_sem, send_sem, recv_sem, mate_send, mate_recv = take(5)

    dp = lax.axis_index('dp')
    core = lax.rem(dp, 2)
    mate = dp + 1 - 2 * core
    py = lax.rem(lax.div(dp, 2), ny)
    pz = lax.div(dp, 2 * ny)

    def at(y, z):
        return (z * ny + y) * 2 + core

    def turn(pos, by, n):
        return lax.rem(pos + by % n, n)

    nbr = {(True, 1): at(turn(py, 1, ny), pz), (True, -1): at(turn(py, -1, ny), pz),
           (False, 1): at(py, turn(pz, 1, nz)), (False, -1): at(py, turn(pz, -1, nz))}

    loads = []
    for j, name in enumerate(names):
        for s in range(n_img):
            loads.append((name, pltpu.make_async_copy(x_in[name].at[s], x_t[name].at[s], ld_sem.at[j, 0, s])))
            loads.append((name, pltpu.make_async_copy(y_in[name].at[s], y_v[name].at[s, 0:TOK, :], ld_sem.at[j, 1, s])))
    vec_load = pltpu.make_async_copy(vec_in, vec_v, ld_sem.at[4, 0, 0])
    for _, ld in loads:
        ld.start()
    vec_load.start()

    barrier = pltpu.get_barrier_semaphore()
    for dev in list(nbr.values()) + [mate]:
        pl.semaphore_signal(barrier, device_id={'dp': dev}, device_id_type=MESH)

    for name in names:
        y_v[name][:, TOK:, :] = jnp.zeros((n_img, KEYS - TOK, y_v[name].shape[2]), BF16)
    pl.semaphore_wait(barrier, 5)

    def ring(i, ph):
        return ny if FIRST_Y[pieces[i][0]] == (ph == 1) else nz

    def place(i, ph):
        return py if FIRST_Y[pieces[i][0]] == (ph == 1) else pz

    def rows1(i, by):
        size = ROWS[pieces[i][0]] // ring(i, 1)
        return pl.ds(pl.multiple_of(turn(place(i, 1), by, ring(i, 1)) * size, 8), size)

    def rows2(i, by):
        big = ROWS[pieces[i][0]] // ring(i, 1)
        size = big // ring(i, 2)
        return pl.ds(pl.multiple_of(place(i, 1) * big + turn(place(i, 2), by, ring(i, 2)) * size, 8), size)

    def view(i, ph, by):
        name, _, col, cols = pieces[i]
        rows = rows1(i, by) if ph == 1 else rows2(i, by)
        return acc[name].at[rows, col:col + cols]

    steps = {}
    for _, typ, i, ph, k in order:
        steps.setdefault((typ, i, ph, k), len(steps))

    def landing(i, ph, k):
        n = ring(i, ph)
        return n - 3 - k if k <= n - 3 else n - 1

    def sent(group, i):
        slots = ((slot1, slot2)[group % 2])[i]
        part = slots.at[0:slots.shape[0] - 1]
        pltpu.make_async_copy(part, part, send_sem.at[group * n_p + i]).wait()

    def copy(typ, i, ph, k):
        way = pieces[i][1] * (1 if typ == 'rs' else -1)
        group = ((0 if typ == 'rs' else 2) + ph - 1) * n_p + i
        slots = (slot1 if ph == 1 else slot2)[i]
        if typ == 'rs':
            src, dst = view(i, ph, -way * (1 + k)), slots.at[k]
        else:
            src = slots.at[landing(i, ph, k - 1)] if k else view(i, ph, 0)
            dst = slots.at[landing(i, ph, k)]
        return pltpu.make_async_remote_copy(src, dst, send_sem.at[group], recv_sem.at[steps[typ, i, ph, k]],
                                            device_id={'dp': nbr[FIRST_Y[pieces[i][0]] == (ph == 1), way]}, device_id_type=MESH)

    def deliver(i, src, by):
        name, _, col, cols = pieces[i]
        if name != 'vec':
            pltpu.make_async_remote_copy(src, mated[name].at[rows1(i, by), col:col + cols], mate_send.at[i], mate_recv.at[i],
                                         device_id={'dp': mate}, device_id_type=MESH).start()

    def multiply(k, name):
        i = next(j for j in range(n_p) if pieces[j][0] == name)
        size = ROWS[name] // ring(i, 1)
        split = PLUS[name] * LANES
        for way, cols in ((1, slice(0, split)), (-1, slice(split, split + MINUS[name] * LANES))):
            idx = lax.rem(place(i, 1) + (2 * ring(i, 1) - way) - way * k, ring(i, 1))
            rows = pl.ds(pl.multiple_of(idx * size, 8), size)
            acc[name][rows, cols] = sum(dot_nn(x_t[name][s, rows, :], y_v[name][s, :, cols]) for s in range(n_img))

    n_first = next(j for j, o in enumerate(order) if o[0] == 'recv')
    begin, todo = order[:n_first], order[n_first:]
    for name in ('vec',) + names:
        if name == 'vec':
            vec_load.wait()
            acc['vec'][...] = vec_v[0] + vec_v[1]
        else:
            for nm, ld in loads:
                if nm == name:
                    ld.wait()
            multiply(0, name)
        for o in begin:
            if pieces[o[2]][0] == name:
                copy(*o[1:]).start()
    for name in names:
        i = next(j for j in range(n_p) if pieces[j][0] == name)
        loop(ring(i, 1) - 1, lambda k, name=name: multiply(k + 1, name))

    for what, typ, i, ph, k in todo:
        if what == 'send':
            copy(typ, i, ph, k).start()
            continue
        copy(typ, i, ph, k).wait_recv()
        way = pieces[i][1] * (1 if typ == 'rs' else -1)
        if typ == 'rs':
            dst = view(i, ph, -way * (2 + k))
            dst[...] = dst[...] + (slot1 if ph == 1 else slot2)[i][k]
        elif ph == 1:
            slot = landing(i, 1, k)
            deliver(i, slot1[i].at[slot], -way * (1 + k))
            if k == 0:
                sent(0, i)
            dst = view(i, 1, -way * (1 + k))
            dst[...] = slot1[i][slot]
        elif k == ring(i, 2) - 2:
            sent(1, i)
            for j in range(ring(i, 2) - 1):
                dst = view(i, 2, -way * (1 + j))
                dst[...] = slot2[i][landing(i, 2, j)]
            deliver(i, view(i, 1, 0), 0)

    for i in range(n_p):
        name, _, col, cols = pieces[i]
        for group in (2, 3):
            sent(group, i)
        whole = acc[name].at[:, col:col + cols]
        if name != 'vec':
            pltpu.make_async_copy(whole, whole, mate_send.at[i]).wait()
            pltpu.make_async_copy(whole, whole, mate_recv.at[i]).wait()


def output_kernel(parts, *refs):
    it = iter(refs)
    take = lambda n: [next(it) for _ in range(n)]
    names = WEIGHTS
    n = len(names)
    own, vec, mated, acts = take(n), next(it), take(n), take(2)
    out, g_vec, g_b, joined = take(n), next(it), next(it), take(2)
    act_v, join_v, sem, act_sem = take(2), take(2), *take(2)
    core = lax.rem(lax.axis_index('dp'), 2)
    copies = []
    for j, name in enumerate(names):
        for c, src in ((core, own[j]), (1 - core, mated[j])):
            rows, cols = src.shape
            step = rows // parts[name]
            for r in range(0, rows, step):
                if name == 'fc2':
                    dst = out[j].at[pl.ds(pl.multiple_of(c * rows + r, 8), step), :]
                else:
                    dst = out[j].at[r:r + step, aligned(c * cols, cols)]
                copies.append(pltpu.make_async_copy(src.at[r:r + step], dst, sem.at[len(copies)]))
    reads = [pltpu.make_async_copy(acts[k], act_v[k], act_sem.at[k]) for k in range(2)]
    writes = [pltpu.make_async_copy(join_v[k], joined[k], act_sem.at[2 + k]) for k in range(2)]
    for c in reads + copies:
        c.start()
    n_vec, width = g_vec.shape
    per = width // LANES
    for i in range(n_vec):
        for t in range(per):
            g_vec[i:i + 1, t * LANES:(t + 1) * LANES] = vec[i * per + t:i * per + t + 1, :]
    for t in range(g_b.shape[1] // LANES):
        g_b[:, t * LANES:(t + 1) * LANES] = vec[n_vec * per + t:n_vec * per + t + 1, :]
    for k in range(2):
        reads[k].wait()
        for m in range(join_v[k].shape[1]):
            join_v[k][:, m, :] = act_v[k][m, 0:join_v[k].shape[0]]
        writes[k].start()
    for c in copies + writes:
        c.wait()


def solution(mesh):
    stages = mesh.shape['pp']
    n_dp = mesh.shape['dp']
    ny = 4 if n_dp == 64 else 2
    nz = n_dp // (2 * ny)
    act_spec = P(None, 'dp')
    stage_spec = P('pp')
    out_act_spec = P('pp', None, 'dp')
    pieces = make_pieces()
    order = make_order(pieces, ny, nz)

    def per_device(x_in, grad_out, vectors, w_qkv, w_proj, w_fc1, b_fc1, w_fc2):
        n_micro, _, seq, width = x_in.shape
        mlp = w_fc1.shape[2]
        heads = w_proj.shape[1]
        x_p = x_in.reshape(n_micro, seq, width).transpose(1, 0, 2)
        go_p = grad_out.reshape(n_micro, seq, width).transpose(1, 0, 2)
        hbm, vmem = pl.BlockSpec(memory_space=pl.ANY), pl.BlockSpec(memory_space=pltpu.VMEM)
        n_img = 2 * n_micro
        act = lambda n, w: jax.ShapeDtypeStruct((n, TOK, w), BF16)
        flat = lambda f: jax.ShapeDtypeStruct((n_img, f, KEYS), BF16)
        dma, vm = pltpu.SemaphoreType.DMA, pltpu.VMEM
        outs = pl.pallas_call(
            functools.partial(pipeline_kernel, (seq, stages, n_micro)),
            name='pipeline',
            out_shape=[act(n_micro, width), act(n_micro, width), flat(width), flat(width), flat(width), flat(mlp // 2),
                       act(n_img, 3 * width // 2), act(n_img, mlp // 2), act(n_img, width // 2),
                       act(n_img, width), jax.ShapeDtypeStruct((2, 256, LANES), F32)],
            in_specs=[hbm, hbm, vmem, vmem, hbm, hbm, hbm, hbm],
            out_specs=[hbm] * 11,
            scratch_shapes=[
                vm((width, 3 * width), BF16), vm((width, width), BF16), vm((width, mlp), BF16), vm((mlp, width), BF16),
                vm((3 * width, width), BF16), vm((width, width), BF16), vm((mlp, width), BF16), vm((width, mlp), BF16),
                vm((n_micro, 3 * width + mlp, KEYS), BF16),
                vm((seq, n_micro, width), BF16), vm((seq, n_micro, width), BF16),
                vm((n_micro, TOK, width), BF16), vm((n_micro, TOK, width), BF16), vm((n_micro, TOK, width), BF16),
                vm((n_micro, TOK, width), BF16), vm((n_micro, TOK, width), BF16), vm((n_micro, KEYS, 3 * width), BF16),
                vm((n_micro, TOK, width), BF16), vm((n_micro, TOK, width), BF16), vm((n_micro, TOK, width), BF16),
                vm((n_micro, TOK, mlp), BF16), vm((n_micro, TOK, mlp), BF16), vm((n_micro, heads, TOK, KEYS), F32),
                vm((n_micro, heads, TOK, KEYS), BF16),
                vm((n_micro, 4, TOK, 1), F32), vm((n_micro, TOK, mlp), BF16), vm((n_micro, TOK, width), BF16),
                vm((KEYS, width), BF16), vm((TOK, width), BF16), vm((n_micro, TOK, 3 * width), BF16),
                vm((2, 2, TOK, KEYS), BF16), vm((2, 2, TOK, KEYS), BF16), vm((KEYS, LANES), F32),
                dma((4,)), dma((2,)), dma((2 * n_micro,)), dma((2 * n_micro,)), dma((n_micro, 10)),
                dma((n_micro, 8)), dma((n_micro, 8)), dma((3,)),
            ],
            compiler_params=pltpu.CompilerParams(collective_id=0, has_side_effects=True, vmem_limit_bytes=67043328),
        )(x_p, go_p, vectors[0], b_fc1, w_qkv[0], w_proj[0].reshape(width, width), w_fc1[0], w_fc2[0])
        so, sg, xa1, xa2, xo, xf, dqkv, dz, dr, gy, vec = outs

        half = {'fc1': mlp // 2, 'fc2': width, 'qkv': 3 * width // 2, 'proj': width // 2}
        feats = {'fc1': width, 'fc2': mlp // 2, 'qkv': width, 'proj': width}
        names = WEIGHTS
        f32 = lambda *s: jax.ShapeDtypeStruct(s, F32)
        slots = [[], []]
        for name, _, _, cols in pieces:
            n1, n2 = (ny, nz) if FIRST_Y[name] else (nz, ny)
            slots[0].append(vm((n1, ROWS[name] // n1, cols), F32))
            slots[1].append(vm((n2, ROWS[name] // (n1 * n2), cols), F32))
        grads = pl.pallas_call(
            functools.partial(grad_kernel, (ny, nz, n_img, pieces, order)),
            name='gradients',
            out_shape=[vm((feats[n], half[n]), F32) for n in names] + [vm((256, LANES), F32)]
            + [vm((feats[n], half[n]), F32) for n in names],
            in_specs=[hbm] * 9,
            out_specs=[vmem] * 9,
            scratch_shapes=(
                [vm((n_img, feats[n], KEYS), BF16) for n in names] + [vm((n_img, KEYS, half[n]), BF16) for n in names]
                + [vm((2, 256, LANES), F32)] + slots[0] + slots[1]
                + [dma((5, 2, n_img)), dma((4 * len(pieces),)), dma((len([o for o in order if o[0] == 'send']),)),
                   dma((len(pieces),)), dma((len(pieces),))]),
            compiler_params=pltpu.CompilerParams(collective_id=1, has_side_effects=True, vmem_limit_bytes=35 * 1024 * 1024),
        )(xa2, xf, xa1, xo, dz, gy, dqkv, dr, vec)
        parts = {'fc1': 3, 'fc2': 3, 'qkv': 3, 'proj': 1}
        raw = jax.ShapeDtypeStruct((seq, n_micro, width), BF16)
        g_fc1, g_fc2, g_qkv, g_proj, g_vectors, g_bfc1, so, sg = pl.pallas_call(
            functools.partial(output_kernel, parts),
            name='outputs',
            out_shape=[f32(width, mlp), f32(mlp, width), f32(width, 3 * width), f32(width, width), f32(vectors.shape[1], width),
                       f32(1, mlp), raw, raw],
            in_specs=[vmem] * 9 + [hbm] * 2,
            out_specs=[hbm] * 4 + [vmem] * 2 + [hbm] * 2,
            scratch_shapes=[vm((n_micro, TOK, width), BF16)] * 2 + [vm((seq, n_micro, width), BF16)] * 2
            + [dma((2 * sum(parts.values()),)), dma((4,))],
            compiler_params=pltpu.CompilerParams(vmem_limit_bytes=5 * 1024 * 1024),
        )(*grads, so, sg)
        so, sg = [t.transpose(1, 0, 2).reshape(1, n_micro, 1, seq, width) for t in (so, sg)]
        return (so, sg, g_vectors[None], g_qkv[None], g_proj.reshape(1, heads, width // heads, width), g_fc1[None], g_bfc1,
                g_fc2[None])

    return jax.shard_map(per_device, mesh=mesh, in_specs=(act_spec, act_spec) + (stage_spec,) * 6,
                         out_specs=(out_act_spec, out_act_spec) + (stage_spec,) * 6, check_vma=False)
```

time: 354 us -> 319 us (0.901)
  local copies, waits for them, and re-layouts: 30.4 us -> 0.65 us
  Pallas kernels: 323 us -> 318 us
    unnamed x18 -> x5, local copies, waits for them, and re-layouts: 24.6 us -> 0.65 us
    pallas_call x1, Pallas kernels: 139 us -> 127 us  [per_device(): pl.pallas_call(functools.partial(pipeline_kernel, (seq, stages, n_micro))...]
    pallas_call x0 -> x1, Pallas kernels: none -> 10.8 us  [per_device(): pl.pallas_call(functools.partial(output_kernel, parts), name='outputs', o...]
    pallas_call x1, Pallas kernels: 184 us -> 180 us  [per_device(): pl.pallas_call(functools.partial(grad_kernel, (ny, nz, n_img, pieces, ord...]
where the time goes in v1:
time: 319 us
  Pallas kernels  318 us (100%)
    pallas_call x1, Pallas kernels, per_device(): pl.pallas_call(functools.partial(grad_kernel, (ny, nz, n_img, pieces, ord...  180 us
    pallas_call x1, Pallas kernels, per_device(): pl.pallas_call(functools.partial(pipeline_kernel, (seq, stages, n_micro))...  127 us
    pallas_call x1, Pallas kernels, per_device(): pl.pallas_call(functools.partial(output_kernel, parts), name='outputs', o...  10.8 us

profile of v1, /device:TPU:1, one launch (start us, length us, event | category | flops | bytes accessed | tf_op | source)
XLA Modules:
  0.0 318.9 jit_solution(6314083330131980947)
XLA Ops:
  0.6 126.6 %pipeline.1 = (bf16[2,208,768]{2,1,0:T(8,128)(2,1)}, bf16[2,208,768]{2,1,0:T(8,128)(2,1)}, bf16[4,768,256]{2,1,0:T(8,128)(2,1)}, bf16[4,768,256]{2,1,0:T(8,128)(...) custom-call(bf16[197,2,768]{2,1,0:T(2,128)(2,1)} %bitcast.27, ...), custom_call_target="tpu_custom_call" | custom-call | tf_op jit(solution)/shard_map/pipeline/pallas_call | solution.py:674
  127.3 0.0 copy-start
  127.3 0.0 copy-start.1
  127.3 180.1 %gradients.1 = (f32[768,1536]{1,0:T(8,128)S(1)}, f32[1536,768]{1,0:T(8,128)S(1)}, f32[768,1152]{1,0:T(8,128)S(1)}, f32[768,384]{1,0:T(8,128)S(1)}, f32[256,128]{...) custom-call(bf16[4,768,256]{2,1,0:T(8,128)(2,1)} %get-tuple-element., ...), custom_call_target="tpu_custom_call" | custom-call | tf_op jit(solution)/shard_map/gradients/pallas_call | solution.py:711
  307.4 0.0 copy-done
  307.4 0.0 copy-done.1
  307.4 10.8 %outputs.1 = (f32[768,3072]{1,0:T(8,128)}, f32[3072,768]{1,0:T(8,128)}, f32[768,2304]{1,0:T(8,128)}, f32[768,768]{1,0:T(8,128)}, f32[9,768]{1,0:T(8,128)S(1)}, /...) custom-call(f32[768,1536]{1,0:T(8,128)S(1)} %get-tuple-element.45.refs_0_, ...), custom_call_target="tpu_custom_call" | custom-call | tf_op jit(solution)/shard_map/outputs/pallas_call | solution.py:727
  318.3 0.6 copy.16
Async XLA Ops:
  127.3 180.1 %copy-start = (bf16[2,208,768]{2,1,0:T(8,128)(2,1)S(1)}, bf16[2,208,768]{2,1,0:T(8,128)(2,1)}, u32[]{:S(2)}) copy-start(bf16[2,208,768]{2,1,0:T(8,128)(2,1)} %get-tuple-element.54.refs_9_) | copy-start | bytes 1916932
  127.3 180.1 %copy-start.1 = (bf16[2,208,768]{2,1,0:T(8,128)(2,1)S(1)}, bf16[2,208,768]{2,1,0:T(8,128)(2,1)}, u32[]{:S(2)}) copy-start(bf16[2,208,768]{2,1,0:T(8,128)(2,1)} %get-tuple-element.55.refs_10_) | copy-start | bytes 1916932

commit v2 on v1

--- a/solution.py
+++ b/solution.py
@@ -369,60 +369,68 @@
 
 
 WEIGHTS = ('fc1', 'fc2', 'qkv', 'proj')
-PIECE_ORDER = ('fc1', 'qkv', 'fc2', 'proj')
-FIRST_Y = {'fc1': True, 'qkv': True, 'fc2': False, 'proj': False, 'vec': True}
-ROWS = {'fc1': 768, 'qkv': 768, 'fc2': 1536, 'proj': 768, 'vec': 256}
-PLUS = {'fc1': 6, 'qkv': 5, 'fc2': 3, 'proj': 2}
-MINUS = {'fc1': 6, 'qkv': 4, 'fc2': 3, 'proj': 1}
-WIDEST = {'fc1': 2, 'qkv': 2, 'fc2': 1, 'proj': 1}
+FIRST_Y = {'vec': True, 'fc1': True, 'qkv': True, 'fc2': False, 'proj': False}
+ROWS = {'vec': 256, 'fc1': 768, 'qkv': 768, 'fc2': 1536, 'proj': 768}
+TILES = {'vec': 1, 'fc1': 12, 'qkv': 9, 'fc2': 6, 'proj': 3}
+WIDEST = {'vec': 1, 'fc1': 2, 'qkv': 2, 'fc2': 1, 'proj': 2}
+WAYS = (1, -1)
 
 
 def make_pieces():
-    pieces = []
-    for name in PIECE_ORDER:
+    pieces, total = [], {}
+    for name, tiles in TILES.items():
+        k = -(-tiles // WIDEST[name])
         col = 0
-        for way, tiles in ((1, PLUS[name]), (-1, MINUS[name])):
-            k = -(-tiles // WIDEST[name])
-            for i in range(k):
-                t = tiles // k + (1 if i < tiles % k else 0)
-                pieces.append((name, way, col * LANES, t * LANES))
-                col += t
-    return pieces + [('vec', 1, 0, LANES)]
-
-
-def make_order(pieces, ny, nz, rate=51.3e3, lat=2.79, lat_y=0.3, first=5.0, ready=15.0, step=0.0736):
-    heap, order, waiting, free, count = [], [], {}, {}, [0]
-
-    def on_y(i, ph):
-        return FIRST_Y[pieces[i][0]] == (ph == 1)
-
-    def ring(i, ph):
-        return ny if on_y(i, ph) else nz
+        for i in range(k):
+            cols = (tiles // k + (i < tiles % k)) * LANES
+            way = min(WAYS, key=lambda w: total.get((FIRST_Y[name], w), 0))
+            total[FIRST_Y[name], way] = total.get((FIRST_Y[name], way), 0) + cols * ROWS[name]
+            pieces.append((name, way, col, cols))
+            col += cols
+    return pieces
+
+
+def ring_of(piece, ph, ny, nz):
+    return ny if FIRST_Y[piece[0]] == (ph == 1) else nz
+
+
+def chain(piece, ph, typ, way, ny, nz):
+    half = ring_of(piece, ph, ny, nz) // 2
+    return half if (way == piece[1]) == (typ == 'rs') else half - 1
+
+
+def make_order(pieces, ny, nz, rate=55.6e3, lat=3.434, first=3.0, ready=11.5, step=0.0626, weights=(1.678, 0.4223, -0.1187, 0.1025, 0.5053)):
+    heap, order, waiting, free, done, ids = [], [], {}, {}, {}, iter(range(10**6))
 
     def nbytes(i, ph):
-        rows = ROWS[pieces[i][0]] // ring(i, 1)
-        return (rows if ph == 1 else rows // ring(i, 2)) * pieces[i][3] * 4
+        rows = ROWS[pieces[i][0]] // ring_of(pieces[i], 1, ny, nz)
+        return (rows if ph == 1 else rows // ring_of(pieces[i], 2, ny, nz)) * pieces[i][3] * 4
 
     def push(t, item):
-        count[0] += 1
-        heapq.heappush(heap, (t, count[0], item))
+        heapq.heappush(heap, (t, next(ids), item))
 
     def dispatch(t, key):
         queue = waiting.get(key)
         if queue and free.get(key, 0.0) <= t + 1e-9:
-            typ, i, ph, k = heapq.heappop(queue)[-1]
-            w = nbytes(i, ph) / rate
+            ev = heapq.heappop(queue)[-1]
+            w = nbytes(ev[1], ev[2]) / rate
             free[key] = t + w
-            order.append(('send', typ, i, ph, k))
+            order.append(('send',) + ev)
             push(t + w, ('free', key))
-            push(t + w + lat + (lat_y if key[0] else 0.0), ('land', (typ, i, ph, k)))
-
-    def enqueue(t, typ, i, ph, k):
-        way = pieces[i][1] * (1 if typ == 'rs' else -1)
-        key = (on_y(i, ph), way)
-        count[0] += 1
-        heapq.heappush(waiting.setdefault(key, []), ((ph == 1 and typ == 'ag', ph == 1, -k if typ == 'rs' else 0, i), count[0], (typ, i, ph, k)))
+            push(t + w + lat, ('land', ev))
+
+    def enqueue(t, *ev):
+        typ, i, ph, way, k = ev
+        key = (FIRST_Y[pieces[i][0]] == (ph == 1), way)
+        rank = (ph == 1, typ == 'ag', ph == 1 and typ == 'ag', k, i / len(pieces))
+        rank = sum(a * b for a, b in zip(weights, rank))
+        heapq.heappush(waiting.setdefault(key, []), (rank, next(ids), ev))
         dispatch(t, key)
+
+    def start(t, typ, i, ph):
+        for way in WAYS:
+            if chain(pieces[i], ph, typ, way, ny, nz):
+                enqueue(t, typ, i, ph, way, 0)
 
     for i in range(len(pieces)):
         push(first, ('start', i))
@@ -432,19 +440,21 @@
         if item[0] == 'free':
             dispatch(t, item[1])
         elif item[0] == 'start':
-            enqueue(t, 'rs', item[1], 1, 0)
+            start(t, 'rs', item[1], 1)
         elif item[0] == 'land':
             seq = max(seq, t) + step
             push(seq, ('done', item[1]))
         else:
-            typ, i, ph, k = item[1]
-            order.append(('recv', typ, i, ph, k))
-            if k < ring(i, ph) - 2:
-                enqueue(t, typ, i, ph, k + 1)
-            elif typ == 'rs':
-                enqueue(t, 'rs' if ph == 1 else 'ag', i, 2, 0)
-            elif ph == 2:
-                enqueue(t, 'ag', i, 1, 0)
+            typ, i, ph, way, k = item[1]
+            order.append(('recv',) + item[1])
+            if k < chain(pieces[i], ph, typ, way, ny, nz) - 1:
+                enqueue(t, typ, i, ph, way, k + 1)
+            done[typ, i, ph] = done.get((typ, i, ph), 0) + 1
+            if done[typ, i, ph] == ring_of(pieces[i], ph, ny, nz) - 1:
+                if typ == 'rs':
+                    start(t, 'rs' if ph == 1 else 'ag', i, 2)
+                elif ph == 2:
+                    start(t, 'ag', i, 1)
     return order
 
 
@@ -462,7 +472,7 @@
     mated = each()
     x_t, y_v = each(), each()
     vec_v = next(it)
-    slot1, slot2 = take(n_p), take(n_p)
+    slots = {(i, ph, way): next(it) for ph in (1, 2) for way in WAYS for i in range(n_p)}
     ld_sem, send_sem, recv_sem, mate_send, mate_recv = take(5)
 
     dp = lax.axis_index('dp')
@@ -484,7 +494,7 @@
     for j, name in enumerate(names):
         for s in range(n_img):
             loads.append((name, pltpu.make_async_copy(x_in[name].at[s], x_t[name].at[s], ld_sem.at[j, 0, s])))
-            loads.append((name, pltpu.make_async_copy(y_in[name].at[s], y_v[name].at[s, 0:TOK, :], ld_sem.at[j, 1, s])))
+            loads.append((name, pltpu.make_async_copy(y_in[name].at[s], y_v[name].at[s], ld_sem.at[j, 1, s])))
     vec_load = pltpu.make_async_copy(vec_in, vec_v, ld_sem.at[4, 0, 0])
     for _, ld in loads:
         ld.start()
@@ -494,117 +504,132 @@
     for dev in list(nbr.values()) + [mate]:
         pl.semaphore_signal(barrier, device_id={'dp': dev}, device_id_type=MESH)
 
-    for name in names:
-        y_v[name][:, TOK:, :] = jnp.zeros((n_img, KEYS - TOK, y_v[name].shape[2]), BF16)
     pl.semaphore_wait(barrier, 5)
 
     def ring(i, ph):
-        return ny if FIRST_Y[pieces[i][0]] == (ph == 1) else nz
+        return ring_of(pieces[i], ph, ny, nz)
+
+    def hops(i, ph, typ, way):
+        return chain(pieces[i], ph, typ, way, ny, nz)
 
     def place(i, ph):
         return py if FIRST_Y[pieces[i][0]] == (ph == 1) else pz
 
-    def rows1(i, by):
+    def rows_of(i, ph, by):
         size = ROWS[pieces[i][0]] // ring(i, 1)
-        return pl.ds(pl.multiple_of(turn(place(i, 1), by, ring(i, 1)) * size, 8), size)
-
-    def rows2(i, by):
-        big = ROWS[pieces[i][0]] // ring(i, 1)
-        size = big // ring(i, 2)
-        return pl.ds(pl.multiple_of(place(i, 1) * big + turn(place(i, 2), by, ring(i, 2)) * size, 8), size)
+        if ph == 1:
+            start = turn(place(i, 1), by, ring(i, 1)) * size
+        else:
+            start, size = place(i, 1) * size, size // ring(i, 2)
+            start = start + turn(place(i, 2), by, ring(i, 2)) * size
+        return pl.ds(pl.multiple_of(start, 8), size)
 
     def view(i, ph, by):
         name, _, col, cols = pieces[i]
-        rows = rows1(i, by) if ph == 1 else rows2(i, by)
-        return acc[name].at[rows, col:col + cols]
-
-    steps = {}
-    for _, typ, i, ph, k in order:
-        steps.setdefault((typ, i, ph, k), len(steps))
-
-    def landing(i, ph, k):
-        n = ring(i, ph)
-        return n - 3 - k if k <= n - 3 else n - 1
-
-    def sent(group, i):
-        slots = ((slot1, slot2)[group % 2])[i]
-        part = slots.at[0:slots.shape[0] - 1]
-        pltpu.make_async_copy(part, part, send_sem.at[group * n_p + i]).wait()
-
-    def copy(typ, i, ph, k):
-        way = pieces[i][1] * (1 if typ == 'rs' else -1)
-        group = ((0 if typ == 'rs' else 2) + ph - 1) * n_p + i
-        slots = (slot1 if ph == 1 else slot2)[i]
+        return acc[name].at[rows_of(i, ph, by), col:col + cols]
+
+    receives = {ev: j for j, ev in enumerate(o[1:] for o in order if o[0] == 'recv')}
+    groups = {key: j for j, key in enumerate((typ, ph, way, i) for typ in ('rs', 'ag') for ph in (1, 2) for way in WAYS
+                                             for i in range(n_p))}
+
+    def landing(i, ph, way, k):
+        n = hops(i, ph, 'ag', way)
+        return slots[i, ph, -way].at[n - 2 - k if k <= n - 2 else n]
+
+    def sent(typ, i, ph):
+        for way in WAYS:
+            n = hops(i, ph, typ, way)
+            if n:
+                part = slots[i, ph, way if typ == 'rs' else -way].at[:n]
+                pltpu.make_async_copy(part, part, send_sem.at[groups[typ, ph, way, i]]).wait()
+
+    def copy(typ, i, ph, way, k):
         if typ == 'rs':
-            src, dst = view(i, ph, -way * (1 + k)), slots.at[k]
+            src, dst = view(i, ph, way * (hops(i, ph, typ, way) - k)), slots[i, ph, way].at[k]
         else:
-            src = slots.at[landing(i, ph, k - 1)] if k else view(i, ph, 0)
-            dst = slots.at[landing(i, ph, k)]
-        return pltpu.make_async_remote_copy(src, dst, send_sem.at[group], recv_sem.at[steps[typ, i, ph, k]],
-                                            device_id={'dp': nbr[FIRST_Y[pieces[i][0]] == (ph == 1), way]}, device_id_type=MESH)
+            src = landing(i, ph, way, k - 1) if k else view(i, ph, 0)
+            dst = landing(i, ph, way, k)
+        dev = nbr[FIRST_Y[pieces[i][0]] == (ph == 1), way]
+        return pltpu.make_async_remote_copy(src, dst, send_sem.at[groups[typ, ph, way, i]], recv_sem.at[receives[typ, i, ph, way, k]],
+                                            device_id={'dp': dev}, device_id_type=MESH)
 
     def deliver(i, src, by):
         name, _, col, cols = pieces[i]
         if name != 'vec':
-            pltpu.make_async_remote_copy(src, mated[name].at[rows1(i, by), col:col + cols], mate_send.at[i], mate_recv.at[i],
+            pltpu.make_async_remote_copy(src, mated[name].at[rows_of(i, 1, by), col:col + cols], mate_send.at[i], mate_recv.at[i],
                                          device_id={'dp': mate}, device_id_type=MESH).start()
 
-    def multiply(k, name):
-        i = next(j for j in range(n_p) if pieces[j][0] == name)
-        size = ROWS[name] // ring(i, 1)
-        split = PLUS[name] * LANES
-        for way, cols in ((1, slice(0, split)), (-1, slice(split, split + MINUS[name] * LANES))):
-            idx = lax.rem(place(i, 1) + (2 * ring(i, 1) - way) - way * k, ring(i, 1))
-            rows = pl.ds(pl.multiple_of(idx * size, 8), size)
-            acc[name][rows, cols] = sum(dot_nn(x_t[name][s, rows, :], y_v[name][s, :, cols]) for s in range(n_img))
+    lead = {name: next(j for j in range(n_p) if pieces[j][0] == name) for name in WEIGHTS}
+
+    def multiply(t, name):
+        i = lead[name]
+        n = ring(i, 1)
+        size = ROWS[name] // n
+        by = (n // 2 - lax.div(t + 1, 2)) * (2 * lax.rem(t, 2) - 1)
+        rows = pl.ds(pl.multiple_of(lax.rem(place(i, 1) + by + n, n) * size, 8), size)
+        acc[name][rows, :] = sum(dot_nn(x_t[name][s, rows, :TOK], y_v[name][s]) for s in range(n_img))
 
     n_first = next(j for j, o in enumerate(order) if o[0] == 'recv')
     begin, todo = order[:n_first], order[n_first:]
-    for name in ('vec',) + names:
-        if name == 'vec':
-            vec_load.wait()
-            acc['vec'][...] = vec_v[0] + vec_v[1]
-        else:
-            for nm, ld in loads:
-                if nm == name:
-                    ld.wait()
-            multiply(0, name)
-        for o in begin:
-            if pieces[o[2]][0] == name:
-                copy(*o[1:]).start()
+    early = 3
+
+    def send_early(name, t):
+        for _, typ, i, ph, way, k in begin:
+            far = hops(i, ph, typ, way) == ring(i, ph) // 2
+            if pieces[i][0] == name and t == (0 if far else WAYS.index(way) + 1):
+                copy(typ, i, ph, way, k).start()
+
+    vec_load.wait()
+    acc['vec'][...] = vec_v[0] + vec_v[1]
+    for t in range(early):
+        send_early('vec', t)
+
+    def compute_early(t):
+        for name in names:
+            @pl.when(t == 0)
+            def _():
+                for nm, ld in loads:
+                    if nm == name:
+                        ld.wait()
+            multiply(t, name)
+            for j in range(early):
+                pl.when(t == j)(functools.partial(send_early, name, j))
+    loop(early, compute_early)
     for name in names:
-        i = next(j for j in range(n_p) if pieces[j][0] == name)
-        loop(ring(i, 1) - 1, lambda k, name=name: multiply(k + 1, name))
-
-    for what, typ, i, ph, k in todo:
+        loop(ring(lead[name], 1) - early, lambda k, name=name: multiply(k + early, name))
+
+    got = {}
+    for what, *ev in todo:
         if what == 'send':
-            copy(typ, i, ph, k).start()
+            copy(*ev).start()
             continue
-        copy(typ, i, ph, k).wait_recv()
-        way = pieces[i][1] * (1 if typ == 'rs' else -1)
+        typ, i, ph, way, k = ev
+        copy(*ev).wait_recv()
+        got[typ, i, ph] = got.get((typ, i, ph), 0) + 1
         if typ == 'rs':
-            dst = view(i, ph, -way * (2 + k))
-            dst[...] = dst[...] + (slot1 if ph == 1 else slot2)[i][k]
+            dst = view(i, ph, way * (hops(i, ph, typ, way) - 1 - k))
+            dst[...] = dst[...] + slots[i, ph, way][k]
         elif ph == 1:
-            slot = landing(i, 1, k)
-            deliver(i, slot1[i].at[slot], -way * (1 + k))
-            if k == 0:
-                sent(0, i)
+            slot = landing(i, 1, way, k)
+            deliver(i, slot, -way * (1 + k))
+            if got[typ, i, ph] == 1:
+                sent('rs', i, 1)
             dst = view(i, 1, -way * (1 + k))
-            dst[...] = slot1[i][slot]
-        elif k == ring(i, 2) - 2:
-            sent(1, i)
-            for j in range(ring(i, 2) - 1):
-                dst = view(i, 2, -way * (1 + j))
-                dst[...] = slot2[i][landing(i, 2, j)]
+            dst[...] = slot[...]
+        elif got[typ, i, ph] == ring(i, 2) - 1:
+            sent('rs', i, 2)
+            for w in WAYS:
+                for j in range(hops(i, 2, 'ag', w)):
+                    dst = view(i, 2, -w * (1 + j))
+                    dst[...] = landing(i, 2, w, j)[...]
             deliver(i, view(i, 1, 0), 0)
 
     for i in range(n_p):
         name, _, col, cols = pieces[i]
-        for group in (2, 3):
-            sent(group, i)
-        whole = acc[name].at[:, col:col + cols]
+        for ph in (1, 2):
+            sent('ag', i, ph)
         if name != 'vec':
+            whole = acc[name].at[:, col:col + cols]
             pltpu.make_async_copy(whole, whole, mate_send.at[i]).wait()
             pltpu.make_async_copy(whole, whole, mate_recv.at[i]).wait()
 
@@ -633,11 +658,11 @@
     writes = [pltpu.make_async_copy(join_v[k], joined[k], act_sem.at[2 + k]) for k in range(2)]
     for c in reads + copies:
         c.start()
-    n_vec, width = g_vec.shape
+    n_vec, _, width = g_vec.shape
     per = width // LANES
     for i in range(n_vec):
         for t in range(per):
-            g_vec[i:i + 1, t * LANES:(t + 1) * LANES] = vec[i * per + t:i * per + t + 1, :]
+            g_vec[i, :, t * LANES:(t + 1) * LANES] = vec[i * per + t:i * per + t + 1, :]
     for t in range(g_b.shape[1] // LANES):
         g_b[:, t * LANES:(t + 1) * LANES] = vec[n_vec * per + t:n_vec * per + t + 1, :]
     for k in range(2):
@@ -703,11 +728,14 @@
         feats = {'fc1': width, 'fc2': mlp // 2, 'qkv': width, 'proj': width}
         names = WEIGHTS
         f32 = lambda *s: jax.ShapeDtypeStruct(s, F32)
-        slots = [[], []]
-        for name, _, _, cols in pieces:
-            n1, n2 = (ny, nz) if FIRST_Y[name] else (nz, ny)
-            slots[0].append(vm((n1, ROWS[name] // n1, cols), F32))
-            slots[1].append(vm((n2, ROWS[name] // (n1 * n2), cols), F32))
+        slots = []
+        for ph in (1, 2):
+            for way in WAYS:
+                for piece in pieces:
+                    rows = ROWS[piece[0]] // ring_of(piece, 1, ny, nz)
+                    rows = rows if ph == 1 else rows // ring_of(piece, 2, ny, nz)
+                    slots.append(vm((chain(piece, ph, 'rs', way, ny, nz) + 1, rows, piece[3]), F32))
+        n_recv = len([o for o in order if o[0] == 'recv'])
         grads = pl.pallas_call(
             functools.partial(grad_kernel, (ny, nz, n_img, pieces, order)),
             name='gradients',
@@ -716,18 +744,17 @@
             in_specs=[hbm] * 9,
             out_specs=[vmem] * 9,
             scratch_shapes=(
-                [vm((n_img, feats[n], KEYS), BF16) for n in names] + [vm((n_img, KEYS, half[n]), BF16) for n in names]
-                + [vm((2, 256, LANES), F32)] + slots[0] + slots[1]
-                + [dma((5, 2, n_img)), dma((4 * len(pieces),)), dma((len([o for o in order if o[0] == 'send']),)),
-                   dma((len(pieces),)), dma((len(pieces),))]),
-            compiler_params=pltpu.CompilerParams(collective_id=1, has_side_effects=True, vmem_limit_bytes=35 * 1024 * 1024),
+                [vm((n_img, feats[n], KEYS), BF16) for n in names] + [vm((n_img, TOK, half[n]), BF16) for n in names]
+                + [vm((2, 256, LANES), F32)] + slots
+                + [dma((5, 2, n_img)), dma((8 * len(pieces),)), dma((n_recv,)), dma((len(pieces),)), dma((len(pieces),))]),
+            compiler_params=pltpu.CompilerParams(collective_id=1, has_side_effects=True, vmem_limit_bytes=37 * 10**6),
         )(xa2, xf, xa1, xo, dz, gy, dqkv, dr, vec)
         parts = {'fc1': 3, 'fc2': 3, 'qkv': 3, 'proj': 1}
         raw = jax.ShapeDtypeStruct((seq, n_micro, width), BF16)
         g_fc1, g_fc2, g_qkv, g_proj, g_vectors, g_bfc1, so, sg = pl.pallas_call(
             functools.partial(output_kernel, parts),
             name='outputs',
-            out_shape=[f32(width, mlp), f32(mlp, width), f32(width, 3 * width), f32(width, width), f32(vectors.shape[1], width),
+            out_shape=[f32(width, mlp), f32(mlp, width), f32(width, 3 * width), f32(width, width), f32(vectors.shape[1], 1, width),
                        f32(1, mlp), raw, raw],
             in_specs=[vmem] * 9 + [hbm] * 2,
             out_specs=[hbm] * 4 + [vmem] * 2 + [hbm] * 2,
@@ -736,7 +763,7 @@
             compiler_params=pltpu.CompilerParams(vmem_limit_bytes=5 * 1024 * 1024),
         )(*grads, so, sg)
         so, sg = [t.transpose(1, 0, 2).reshape(1, n_micro, 1, seq, width) for t in (so, sg)]
-        return (so, sg, g_vectors[None], g_qkv[None], g_proj.reshape(1, heads, width // heads, width), g_fc1[None], g_bfc1,
+        return (so, sg, g_vectors.transpose(1, 0, 2), g_qkv[None], g_proj.reshape(1, heads, width // heads, width), g_fc1[None], g_bfc1,
                 g_fc2[None])
 
     return jax.shard_map(per_device, mesh=mesh, in_specs=(act_spec, act_spec) + (stage_spec,) * 6,

time: 319 us -> 308 us (0.966)
  Pallas kernels: 318 us -> 307 us
    pallas_call x1, Pallas kernels: 180 us -> 169 us  [per_device(): pl.pallas_call(functools.partial(grad_kernel, (ny, nz, n_img, pieces, ord...]
where the time goes in v2:
time: 308 us; the launch traced here: 307 us
  Pallas kernels  307 us (100%)
    pallas_call x1, Pallas kernels, per_device(): pl.pallas_call(functools.partial(grad_kernel, (ny, nz, n_img, pieces, ord...  169 us
    pallas_call x1, Pallas kernels, per_device(): pl.pallas_call(functools.partial(pipeline_kernel, (seq, stages, n_micro))...  127 us
    pallas_call x1, Pallas kernels, per_device(): pl.pallas_call(functools.partial(output_kernel, parts), name='outputs', o...  10.9 us

profile of v2, /device:TPU:1, one launch (start us, length us, event | category | flops | bytes accessed | tf_op | source)
XLA Modules:
  0.0 307.5 jit_solution(3034738660120273481)
XLA Ops:
  0.6 126.6 %pipeline.1 = (bf16[2,208,768]{2,1,0:T(8,128)(2,1)}, bf16[2,208,768]{2,1,0:T(8,128)(2,1)}, bf16[4,768,256]{2,1,0:T(8,128)(2,1)}, bf16[4,768,256]{2,1,0:T(8,128)(...) custom-call(bf16[197,2,768]{2,1,0:T(2,128)(2,1)} %bitcast.26, ...), custom_call_target="tpu_custom_call" | custom-call | tf_op jit(solution)/shard_map/pipeline/pallas_call | solution.py:699
  127.3 0.0 copy-start
  127.3 0.0 copy-start.1
  127.3 169.1 %gradients.1 = (f32[768,1536]{1,0:T(8,128)S(1)}, f32[1536,768]{1,0:T(8,128)S(1)}, f32[768,1152]{1,0:T(8,128)S(1)}, f32[768,384]{1,0:T(8,128)S(1)}, f32[256,128]{...) custom-call(bf16[4,768,256]{2,1,0:T(8,128)(2,1)} %get-tuple-element., ...), custom_call_target="tpu_custom_call" | custom-call | tf_op jit(solution)/shard_map/gradients/pallas_call | solution.py:739
  296.4 0.0 copy-done
  296.4 0.0 copy-done.1
  296.5 10.9 %outputs.1 = (f32[768,3072]{1,0:T(8,128)}, f32[3072,768]{1,0:T(8,128)}, f32[768,2304]{1,0:T(8,128)}, f32[768,768]{1,0:T(8,128)}, f32[9,1,768]{2,1,0:T(1,128)}, /...) custom-call(f32[768,1536]{1,0:T(8,128)S(1)} %get-tuple-element.45.refs_0_, ...), custom_call_target="tpu_custom_call" | custom-call | tf_op jit(solution)/shard_map/outputs/pallas_call | solution.py:754
Async XLA Ops:
  127.3 169.2 %copy-start = (bf16[2,208,768]{2,1,0:T(8,128)(2,1)S(1)}, bf16[2,208,768]{2,1,0:T(8,128)(2,1)}, u32[]{:S(2)}) copy-start(bf16[2,208,768]{2,1,0:T(8,128)(2,1)} %get-tuple-element.54.refs_9_) | copy-start | bytes 1916932
  127.3 169.2 %copy-start.1 = (bf16[2,208,768]{2,1,0:T(8,128)(2,1)S(1)}, bf16[2,208,768]{2,1,0:T(8,128)(2,1)}, u32[]{:S(2)}) copy-start(bf16[2,208,768]{2,1,0:T(8,128)(2,1)} %get-tuple-element.55.refs_10_) | copy-start | bytes 1916932
